TPU v7x, 512 devices: a whole 4x8x8 slice. The times are simulated.
512 devices in a mesh: tm: 128 (over z, y, core), pair: 4 (over x).
Axes of the slice: x: 4, y: 8, z: 8, core: 2. Of those that a mesh axis runs over, the one named last changes fastest.
Arguments:
- x_series: float32 [128, 524288], P('pair', 'tm'), may hold values from -6 to 6
- y_series: float32 [128, 524288], P('pair', 'tm'), may hold values from -6 to 6
Outputs:
- correlation: float32 [128, 512], P('tm', 'pair')
All inputs are finite; a program needn't handle non-finite values.
Results may differ from a plain program's by a relative error of at most 0.000082.
Values sent between devices are 32-bit elements; how exact they have to be, the bound alone decides.
A program may use at most 64 MiB of HBM per device.

v0:
```python
import math

import jax
import jax.numpy as jnp
from jax import lax
from jax.sharding import Mesh
from jax.sharding import PartitionSpec as P

L = 512
TM = ("tm_0", "tm_1", "tm_2")


def passed_along(array, axis, by):
    devices = lax.axis_size(axis)
    pairs = [(i, i + by) for i in range(devices) if 0 <= i + by < devices]
    return lax.ppermute(array, axis, pairs)


def rows_for(lines, devices):
    spare = -lines.shape[0] % devices
    if not spare:
        return lines
    return jnp.concatenate([lines, jnp.zeros((spare, *lines.shape[1:]), lines.dtype)])


def from_everyone(array, axis):
    copies = jnp.broadcast_to(array, (lax.axis_size(axis), *array.shape))
    return lax.all_to_all(copies, axis, split_axis=0, concat_axis=0, tiled=True)


def laid_out(blocks, dim):
    lengths = list(blocks.shape[1:])
    lengths[dim] *= blocks.shape[0]
    return jnp.moveaxis(blocks, 0, dim).reshape(lengths)


def gathered_by_axis(array, axes, dim):
    far, near = axes
    blocks = from_everyone(from_everyone(array, far), near)
    return laid_out(blocks.swapaxes(0, 1).reshape(-1, *array.shape), dim)


def cut_along(array, dim, devices):
    before, after = (array.shape[:dim], array.shape[dim + 1 :])
    return jnp.moveaxis(array.reshape(*before, devices, -1, *after), dim, 0)


def sent_and_summed(array, axis, dim):
    devices = lax.axis_size(axis)
    blocks = lax.all_to_all(cut_along(array, dim, devices), axis, 0, 0, tiled=True)
    return jnp.sum(blocks, axis=0)


def sum_by_axis(array, axes, dim):
    far, near = axes
    own = sent_and_summed(cut_along(array, dim, lax.axis_size(far)), near, dim + 1)
    return jnp.sum(lax.all_to_all(own, far, 0, 0, tiled=True), axis=0)


def nested_sum(array, axes):
    lines = array.reshape(-1)
    padded = rows_for(lines, lax.axis_size(axes[0]) * lax.axis_size(axes[1]))
    whole = gathered_by_axis(sum_by_axis(padded, axes, 0), axes, 0)
    return lax.slice_in_dim(whole, 0, len(lines)).reshape(array.shape)


def lag_products(series, extended):
    block_len = min(128, L)
    pair_count, length = series.shape
    block_rows = length // block_len
    left_rows = series.reshape(pair_count, block_rows, block_len)
    pieces = [
        extended[:, offset * block_len : offset * block_len + length].reshape(
            pair_count, block_rows, block_len
        )
        for offset in range(L // block_len + 1)
    ]
    right_rows = jnp.concatenate(pieces, axis=2)
    grams = jnp.einsum(
        "pbi,pbj->pij",
        left_rows,
        right_rows,
        precision=lax.Precision.HIGHEST,
        preferred_element_type=jnp.float32,
    )
    span_cols = L + block_len
    flattened = grams.reshape(pair_count, block_len * span_cols)
    flattened = jnp.pad(flattened, ((0, 0), (0, block_len)))
    skewed = flattened.reshape(pair_count, block_len, span_cols + 1)
    return jnp.sum(skewed[:, :, :L], axis=1)


def per_block(members):
    return lag_products(members[0], members[1])


def body(x_series, y_series):
    head_rows = y_series[:, :L]
    incoming = passed_along(head_rows, TM, -1)
    extended = jnp.concatenate([y_series, incoming], axis=1)
    pairs_here, length = x_series.shape
    group_size = min(32, pairs_here)
    block_count = pairs_here // group_size
    partial_value = lax.map(
        per_block,
        (
            x_series.reshape(block_count, group_size, length),
            extended.reshape(block_count, group_size, length + L),
        ),
    )
    partial_value = partial_value.reshape(pairs_here, L)
    norm_scale = 1.0 / math.sqrt(lax.axis_size(TM) * length)
    summed = nested_sum(partial_value, (("tm_0", "tm_1"), "tm_2"))
    regrouped = lax.all_to_all(summed, "pair", split_axis=1, concat_axis=0, tiled=True)
    share_rows = regrouped.shape[0] // lax.axis_size(TM)
    lagged = lax.dynamic_slice_in_dim(regrouped, lax.axis_index(TM) * share_rows, share_rows, 0)
    return lagged * norm_scale


def solution(mesh):
    split = Mesh(
        mesh.devices.reshape(8, 8, 2, mesh.shape["pair"]), ("tm_0", "tm_1", "tm_2", "pair")
    )
    return jax.shard_map(
        body,
        mesh=split,
        in_specs=(P("pair", TM), P("pair", TM)),
        out_specs=P(TM, "pair"),
        check_vma=False,
    )
```

profile of v0, /device:TPU:1, one launch (start us, length us, event | category | flops | bytes accessed | tf_op | source)
XLA Modules:
  0.0 129.0 jit_solution(14724607934596769596)
XLA Ops:
  0.0 0.8 slice.25
  0.8 8.7 %collective-permute-start = (f32[32,512]{1,0:T(8,128)S(1)}, f32[32,512]{1,0:T(8,128)S(1)}, u32[]{:S(2)}, u32[]{:S(2)}) collective-permute-start(f32[32,512]{1,0:T(8,128)S(1)} %slice.25), channel_id=1, source_target_pairs={{4,0},{8,4},{12,8},{16,12},{20,16},{24,20},{28,24},{32,28},{36,32}... | collective-permute-start | bytes 196616 | tf_op jit(solution)/shard_map/ppermute | solution.py:16
  9.6 1.1 constant_dynamic-update-slice_fusion.1
  10.7 1.1 copy.13
  11.8 1.1 copy.18
  13.0 0.0 collective-permute-done
  13.0 0.1 slice_bitcast_fusion
  13.2 0.1 copy.14
  13.3 0.1 copy.15
  13.4 0.1 copy.16
  13.5 0.1 copy.17
  13.8 19.0 %convolution_bitcast_fusion = f32[32,128,640]{1,2,0:T(8,128)} fusion(f32[32,32,640]{2,1,0:T(8,128)S(1)} %constant_dynamic-update-slice_fusion.2, f32[32,32,128]{2,1,0:T(8,128)S(1)} %bitcast.39), kind=kOutput, calls=%fused_computation.1 | convolution fusion | flops 1006632960 | bytes 13631488 | tf_op jit(solution)/shard_map/while/body/eval_jaxpr/pbi,pbj->pij/dot_general | solution.py:79
  32.8 12.2 %copy.19 = f32[4,8,128,640]{3,1,2,0:T(8,128)} copy(f32[4,8,128,640]{2,3,1,0:T(8,128)} %bitcast.31) | data formatting | bytes 20971520
  45.0 8.6 %pad.5 = f32[32,82048]{1,0:T(8,128)} pad(f32[32,81920]{1,0:T(8,128)} %bitcast.32, f32[]{:T(128)} %constant.13.clone.1), padding=0_0x0_128 | pad | bytes 20987908 | tf_op jit(solution)/shard_map/while/body/eval_jaxpr/jit(_pad)/pad | solution.py:88
  53.5 14.9 %reshape.57 = f32[32,128,641]{2,1,0:T(8,128)} reshape(f32[32,82048]{1,0:T(8,128)} %pad.5) | data formatting | bytes 21004288 | tf_op jit(solution)/shard_map/while/body/eval_jaxpr/reshape | solution.py:89
  68.5 4.5 %slice_reduce_fusion = f32[32,512]{1,0:T(8,128)S(1)} fusion(f32[32,128,641]{2,1,0:T(8,128)} %reshape.57), kind=kLoop, calls=%fused_computation | loop fusion | flops 2080768 | bytes 8454144 | tf_op jit(solution)/shard_map/while/body/eval_jaxpr/reduce_sum | solution.py:90
  73.0 3.4 %all_to_all.47 = f32[2,64,128]{2,1,0:T(8,128)S(1)} all-to-all(f32[2,64,128]{2,1,0:T(8,128)S(1)} %copy.10), channel_id=1, replica_groups=mesh['tm_0'=8,'tm_1'=8,'tm_2'=2,'pair'=4] {'tm_2'}, dimensions={0} | all-to-all | bytes 131072 | tf_op jit(solution)/shard_map/all_to_all | solution.py:50
  76.5 21.6 %all_to_all.48 = f32[64,1,128]{2,1,0:T(1,128)S(1)} all-to-all(f32[64,1,128]{2,1,0:T(1,128)S(1)} %bitcast.44), channel_id=1, replica_groups=mesh['tm_0'=8,'tm_1'=8,'tm_2'=2,'pair'=4] {'tm_0','tm_1'}, dimensions={0} | all-to-all | bytes 65536 | tf_op jit(solution)/shard_map/all_to_all | solution.py:57
  98.1 0.1 reduce_sum.30
  98.2 14.7 %all_to_all.49 = f32[64,1,128]{2,1,0:T(1,128)S(1)} all-to-all(f32[64,1,128]{2,1,0:T(1,128)S(1)} %broadcast_in_dim.10), channel_id=1, replica_groups=mesh['tm_0'=8,'tm_1'=8,'tm_2'=2,'pair'=4] {'tm_0','tm_1'}, dimensions={0} | all-to-all | bytes 65536 | tf_op jit(solution)/shard_map/all_to_all | solution.py:28
  112.9 6.4 %all_to_all.50 = f32[2,64,128]{2,1,0:T(8,128)S(1)} all-to-all(f32[2,64,128]{2,1,0:T(8,128)S(1)} %broadcast_in_dim.11), channel_id=1, replica_groups=mesh['tm_0'=8,'tm_1'=8,'tm_2'=2,'pair'=4] {'tm_2'}, dimensions={0} | all-to-all | bytes 131072 | tf_op jit(solution)/shard_map/all_to_all | solution.py:28
  119.3 0.1 copy.11
  119.3 0.6 copy.12
  120.0 4.0 %all-to-all-start.4 = ((f32[32,4,128]{2,0,1:T(8,128)}), f32[32,4,128]{2,0,1:T(8,128)S(1)}, u32[]{:S(2)}, u32[]{:S(2)}) async-start(f32[32,4,128]{2,0,1:T(8,128)} %copy.12), calls=%async_computation.4 | async-start | bytes 131072 | tf_op jit(solution)/shard_map/all_to_all | solution.py:114
  124.0 4.5 %all-to-all-done.4 = f32[32,4,128]{2,0,1:T(8,128)S(1)} async-done(((f32[32,4,128]{2,0,1:T(8,128)}), f32[32,4,128]{2,0,1:T(8,128)S(1)}, u32[]{:S(2)}, u32[]{:S(2)}) %all-to-all-start.4) | async-done | bytes 65568 | tf_op jit(solution)/shard_map/all_to_all | solution.py:114
  128.5 0.5 dynamic-slice_multiply_fusion
  (11 shorter events, 0.3 us)
Async XLA Ops:
  0.8 12.2 %collective-permute-start = (f32[32,512]{1,0:T(8,128)S(1)}, f32[32,512]{1,0:T(8,128)S(1)}, u32[]{:S(2)}, u32[]{:S(2)}) collective-permute-start(f32[32,512]{1,0:T(8,128)S(1)} %slice.25), channel_id=1, source_target_pairs={{4,0},{8,4},{12,8},{16,12},{20,16},{24,20},{28,24},{32,28},{36,32}... | collective-permute-start | bytes 196616 | tf_op jit(solution)/shard_map/ppermute | solution.py:16
  120.0 8.5 %all-to-all-start.4 = ((f32[32,4,128]{2,0,1:T(8,128)}), f32[32,4,128]{2,0,1:T(8,128)S(1)}, u32[]{:S(2)}, u32[]{:S(2)}) async-start(f32[32,4,128]{2,0,1:T(8,128)} %copy.12), calls=%async_computation.4 | async-start | bytes 131072 | tf_op jit(solution)/shard_map/all_to_all | solution.py:114
where the time goes:
time: 130 us; the launch traced here: 129 us
  blocking collectives  46.1 us (35%)
  local copies, waits for them, and re-layouts  41.4 us (32%)
  matrix products  19 us (15%)
  starting transfers between devices  12.7 us (10%)
  other arithmetic  5.13 us (4%)
  waiting for transfers between devices  4.48 us (3%)
    all_to_all x1, blocking collectives, sum_by_axis(): return jnp.sum(lax.all_to_all(own, far, 0, 0, tiled=True), axis=0)  21.6 us
    all_to_all x2, blocking collectives, from_everyone(): return lax.all_to_all(copies, axis, split_axis=0, concat_axis=0, tiled=True)  21 us
    dot_general x1, matrix products, lag_products(): jnp.einsum('pbi,pbj->pij', left_rows, right_rows, precision=lax.Precision...  19 us
    unnamed x13, local copies, waits for them, and re-layouts  16.2 us
    reshape x1, local copies, waits for them, and re-layouts, lag_products(): skewed = flattened.reshape(pair_count, block_len, span_cols + 1)  14.9 us
    ppermute x1, starting transfers between devices, passed_along(): return lax.ppermute(array, axis, pairs)  8.73 us
    pad x1, local copies, waits for them, and re-layouts, lag_products(): flattened = jnp.pad(flattened, ((0, 0), (0, block_len)))  8.56 us
    reduce_sum x1, other arithmetic, lag_products(): return jnp.sum(skewed[:, :, :L], axis=1)  4.52 us
  transfers between devices with their start and end apart: 2, of which 1 were waited for; matrix products, arithmetic and copies ran while one was open for 3% of the time, Pallas kernels for 0%

commit v1 on v0

v1 whole, which is shorter than its diff:
```python
import functools
import math

import jax
import jax.numpy as jnp
import ml_dtypes
import numpy as np
from jax import lax
from jax.experimental import pallas as pl
from jax.experimental.pallas import tpu as pltpu
from jax.sharding import PartitionSpec as P

L = 512
BLK = 256
N = 768
F = N // 2
MESH = pl.DeviceIdType.MESH


def halves(array):
    high = array.astype(ml_dtypes.bfloat16)
    low = (array - high.astype(np.float64)).astype(ml_dtypes.bfloat16)
    return high, low


@functools.cache
def tables(total):
    theta = 2 * np.pi * (np.arange(F) + 0.5) / N
    sample, lag = np.arange(BLK), np.arange(L)
    forward = np.concatenate(
        [np.cos(np.outer(sample, theta)), np.sin(np.outer(sample, theta))], axis=1
    )
    backward = np.concatenate(
        [np.cos(np.outer(theta, lag)), -np.sin(np.outer(theta, lag))], axis=0
    ) * (2.0 / N / math.sqrt(total))
    high, low = halves(forward)
    fwd = np.concatenate([high, high, low], axis=0)
    high, low = halves(backward)
    bwd = np.concatenate([high, high, low], axis=0)
    once, twice = np.exp(-1j * theta * BLK), np.exp(-2j * theta * BLK)
    turns = np.zeros((8, F), np.float32)
    turns[0], turns[1], turns[2], turns[3] = once.real, once.imag, twice.real, twice.imag
    return fwd, bwd, turns


def split_in(value, ref, row, width):
    high = value.astype(jnp.bfloat16)
    low = (value - high.astype(jnp.float32)).astype(jnp.bfloat16)
    rows = value.shape[0]
    ref[row : row + rows, 0:width] = high
    ref[row : row + rows, width : 2 * width] = low
    ref[row : row + rows, 2 * width : 3 * width] = high


def kernel(
    sizes, x_hbm, y_hbm, fwd_hbm, bwd_hbm, turns_hbm, out_ref,
    xv, yv, head, fwd, bwd, turns, parts, fx, fy, res, rparts,
    send_a, recv_a, send_b, recv_b,
    load_sem, halo_sem, sa_sem, ra_sem, sb_sem, rb_sem,
):
    zs, ys, xs = sizes
    pairs, length = xv.shape
    blocks = length // BLK
    extra = L // BLK
    group = 2 * ys
    depth = zs // xs
    tm, mx = lax.axis_index("tm"), lax.axis_index("pair")
    mz, mg = tm // group, tm % group
    my, mc = mg // 2, mg % 2
    steps = [ys // 2]
    for d in range(ys // 2 - 1, 0, -1):
        steps += [d, ys - d]
    peers = [(d, c) for d in steps for c in (0, 1)] + [(0, 1)]

    def peer(d, c):
        return ((my + d) % ys) * 2 + (mc + c) % 2

    loads = [
        pltpu.make_async_copy(x_hbm, xv, load_sem.at[0]),
        pltpu.make_async_copy(fwd_hbm, fwd, load_sem.at[1]),
        pltpu.make_async_copy(y_hbm, yv, load_sem.at[2]),
        pltpu.make_async_copy(turns_hbm, turns, load_sem.at[3]),
        pltpu.make_async_copy(bwd_hbm, bwd, load_sem.at[4]),
    ]
    for load in loads:
        load.start()

    barrier = pltpu.get_barrier_semaphore()
    last = zs * group - 1

    @pl.when(tm < last)
    def _():
        pl.semaphore_signal(
            barrier, inc=1, device_id=(tm + 1, mx), device_id_type=MESH
        )

    source_x = mz // depth
    for z in range(zs):

        @pl.when(jnp.logical_or(source_x != mx, z != mz))
        def _():
            pl.semaphore_signal(
                barrier, inc=1, device_id=(z * group + mg, source_x), device_id_type=MESH
            )

    for d, c in peers:
        pl.semaphore_signal(
            barrier, inc=1, device_id=(mz * group + peer(d, c), mx), device_id_type=MESH
        )

    loads[0].wait()
    for j in range(blocks):
        split_in(xv[:, j * BLK : (j + 1) * BLK], parts, j * pairs, BLK)
    loads[1].wait()
    fx[...] = jnp.dot(
        parts[0 : blocks * pairs, :], fwd[...], preferred_element_type=jnp.float32
    )

    own = jnp.where(source_x == mx, 1, 0)
    wanted = (group - 1) + depth * xs - own + jnp.where(tm > 0, 1, 0)
    pl.semaphore_wait(barrier, wanted)
    loads[2].wait()
    halo = pltpu.make_async_remote_copy(
        src_ref=yv.at[:, 0:L],
        dst_ref=head,
        send_sem=halo_sem.at[0],
        recv_sem=halo_sem.at[1],
        device_id=(jnp.maximum(tm - 1, 0), mx),
        device_id_type=MESH,
    )

    @pl.when(tm > 0)
    def _():
        halo.start()

    @pl.when(tm == last)
    def _():
        head[...] = jnp.zeros_like(head)

    for j in range(blocks):
        split_in(yv[:, j * BLK : (j + 1) * BLK], parts, j * pairs, BLK)
    fy[0 : blocks * pairs, :] = jnp.dot(
        parts[0 : blocks * pairs, :], fwd[...], preferred_element_type=jnp.float32
    )
    loads[3].wait()

    def take(ref, block, at, c):
        rows = pl.ds(pl.multiple_of(block * pairs + at, 8), 8)
        return ref[rows, c * 128 : (c + 1) * 128], ref[rows, F + c * 128 : F + (c + 1) * 128]

    def turn(which, c):
        lanes = slice(c * 128, (c + 1) * 128)
        real, imag = turns[2 * which : 2 * which + 1, lanes], turns[2 * which + 1 : 2 * which + 2, lanes]
        return real, imag

    def products(at, c, first, terms):
        xs_ = {i: take(fx, i, at, c) for i in sorted({i for i, _ in terms})} if not first else {}
        sums = {}
        for i, j in terms:
            cx, sx = xs_[i] if i in xs_ else take(fx, i, at, c)
            cy, sy = take(fy, j, at, c)
            real, imag = cx * cy + sx * sy, sx * cy - cx * sy
            if j - i in sums:
                a, b = sums[j - i]
                real, imag = real + a, imag + b
            sums[j - i] = (real, imag)
        total_real = total_imag = None
        for shift, (real, imag) in sums.items():
            if shift > 0:
                a, b = turn(shift - 1, c)
                real, imag = real * a - imag * b, real * b + imag * a
            total_real = real if total_real is None else total_real + real
            total_imag = imag if total_imag is None else total_imag + imag
        return total_real, total_imag

    near = [(i, i + s) for i in range(blocks) for s in range(extra + 1) if i + s < blocks]
    far = [(i, i + s) for i in range(blocks) for s in range(extra + 1) if i + s >= blocks]

    @pl.loop(0, pairs // 8)
    def _(g):
        at = pl.multiple_of(g * 8, 8)
        for c in range(F // 128):
            real, imag = products(at, c, True, near)
            res[pl.ds(at, 8), c * 128 : (c + 1) * 128] = real
            res[pl.ds(at, 8), F + c * 128 : F + (c + 1) * 128] = imag

    @pl.when(tm < last)
    def _():
        halo.wait_recv()

    for j in range(extra):
        split_in(head[:, j * BLK : (j + 1) * BLK], parts, j * pairs, BLK)
    fy[blocks * pairs : (blocks + extra) * pairs, :] = jnp.dot(
        parts[0 : extra * pairs, :], fwd[...], preferred_element_type=jnp.float32
    )
    for g in range(pairs // 8):
        for c in range(F // 128):
            real, imag = products(g * 8, c, False, far)
            res[g * 8 : g * 8 + 8, c * 128 : (c + 1) * 128] += real
            res[g * 8 : g * 8 + 8, F + c * 128 : F + (c + 1) * 128] += imag

    split_in(res[...], rparts, 0, N)
    loads[4].wait()
    lagged = jnp.dot(rparts[...], bwd[...], preferred_element_type=jnp.float32)
    for e in range(depth):
        for q in range(xs):
            send_a[:, e * xs + q, :] = lagged[
                e * group : (e + 1) * group, q * 128 : (q + 1) * 128
            ]

    def copy_a(at, slot):
        return pltpu.make_async_remote_copy(
            src_ref=send_a.at[at],
            dst_ref=recv_a.at[slot],
            send_sem=sa_sem.at[at],
            recv_sem=ra_sem.at[slot],
            device_id=(mz * group + at, mx),
            device_id_type=MESH,
        )

    for d, c in peers:
        copy_a(peer(d, c), mg).start()
    total = send_a[mg]
    for d, c in reversed(peers):
        at = peer(d, c)
        copy_a(at, at).wait_recv()
        total = total + recv_a[at]
    for i in range(depth * xs):
        send_b[i] = total[i : i + 1, :]

    def copy_b(i, slot):
        z, q = mx * depth + i // xs, i % xs
        return pltpu.make_async_remote_copy(
            src_ref=send_b.at[i],
            dst_ref=recv_b.at[slot],
            send_sem=sb_sem.at[i],
            recv_sem=rb_sem.at[slot],
            device_id=(z * group + mg, q),
            device_id_type=MESH,
        )

    def is_own(i):
        return jnp.logical_and(mx * depth + i // xs == mz, i % xs == mx)

    for i in range(depth * xs):

        @pl.when(jnp.logical_not(is_own(i)))
        def _():
            copy_b(i, mz).start()

        @pl.when(is_own(i))
        def _():
            recv_b[mz] = send_b[i]

    for z in range(zs):

        @pl.when(jnp.logical_or(source_x != mx, z != mz))
        def _():
            copy_b(0, z).wait_recv()

    value = recv_b[0]
    for z in range(1, zs):
        value = value + recv_b[z]
    out_ref[...] = value

    @pl.when(tm > 0)
    def _():
        halo.wait_send()

    for d, c in peers:
        copy_a(peer(d, c), mg).wait_send()
    for i in range(depth * xs):

        @pl.when(jnp.logical_not(is_own(i)))
        def _():
            copy_b(i, mz).wait_send()


def body(sizes, total, x_series, y_series):
    fwd, bwd, turns = tables(total)
    zs, ys, xs = sizes
    pairs, length = x_series.shape
    group, depth = 2 * ys, zs // xs
    blocks, extra = length // BLK, L // BLK
    f32, bf16 = jnp.float32, jnp.bfloat16
    dma = pltpu.SemaphoreType.DMA
    return pl.pallas_call(
        functools.partial(kernel, sizes),
        out_shape=jax.ShapeDtypeStruct((1, L // xs), f32),
        in_specs=[pl.BlockSpec(memory_space=pl.ANY)] * 5,
        out_specs=pl.BlockSpec(memory_space=pltpu.VMEM),
        scratch_shapes=[
            pltpu.VMEM((pairs, length), f32),
            pltpu.VMEM((pairs, length), f32),
            pltpu.VMEM((pairs, L), f32),
            pltpu.VMEM(fwd.shape, bf16),
            pltpu.VMEM(bwd.shape, bf16),
            pltpu.VMEM(turns.shape, f32),
            pltpu.VMEM((blocks * pairs, 3 * BLK), bf16),
            pltpu.VMEM((blocks * pairs, N), f32),
            pltpu.VMEM(((blocks + extra) * pairs, N), f32),
            pltpu.VMEM((pairs, N), f32),
            pltpu.VMEM((pairs, 3 * N), bf16),
            pltpu.VMEM((group, depth * xs, L // xs), f32),
            pltpu.VMEM((group, depth * xs, L // xs), f32),
            pltpu.VMEM((depth * xs, 1, L // xs), f32),
            pltpu.VMEM((zs, 1, L // xs), f32),
            dma((5,)),
            dma((2,)),
            dma((group,)),
            dma((group,)),
            dma((depth * xs,)),
            dma((zs,)),
        ],
        compiler_params=pltpu.CompilerParams(
            collective_id=0, has_side_effects=True
        ),
    )(x_series, y_series, jnp.asarray(fwd), jnp.asarray(bwd), jnp.asarray(turns))


def solution(mesh):
    sizes = (8, 8, mesh.shape["pair"])
    total = 524288
    return jax.shard_map(
        functools.partial(body, sizes, total),
        mesh=mesh,
        in_specs=(P("pair", "tm"), P("pair", "tm")),
        out_specs=P("tm", "pair"),
        check_vma=False,
    )
```

time: 130 us -> 28 us (0.22)
  blocking collectives: 46.1 us -> 0 us
  local copies, waits for them, and re-layouts: 41.4 us -> 1.19 us
  Pallas kernels: 0 us -> 26.5 us
  matrix products: 19 us -> 0 us
  starting transfers between devices: 12.7 us -> 0 us
  other arithmetic: 5.13 us -> 0 us
  waiting for transfers between devices: 4.48 us -> 0 us
    all_to_all x4 -> x0, blocking collectives: 46.1 us -> none  [the longest x1 21.6 us: sum_by_axis(): return jnp.sum(lax.all_to_all(own, far, 0, 0, tiled=True), axis=0)]
    pallas_call x0 -> x1, Pallas kernels: none -> 26.5 us  [body(): pl.pallas_call(functools.partial(kernel, sizes), out_shape=jax.ShapeDtype...]
    dot_general x1 -> x0, matrix products: 19 us -> none  [lag_products(): jnp.einsum('pbi,pbj->pij', left_rows, right_rows, precision=lax.Precision...]
    unnamed x13 -> x1, local copies, waits for them, and re-layouts: 16.2 us -> 1.19 us
    reshape x1 -> x0, local copies, waits for them, and re-layouts: 14.9 us -> none  [lag_products(): skewed = flattened.reshape(pair_count, block_len, span_cols + 1)]
    ppermute x1 -> x0, starting transfers between devices: 8.73 us -> none  [passed_along(): return lax.ppermute(array, axis, pairs)]
    pad x1 -> x0, local copies, waits for them, and re-layouts: 8.56 us -> none  [lag_products(): flattened = jnp.pad(flattened, ((0, 0), (0, block_len)))]
    reduce_sum x3 -> x0, other arithmetic: 4.61 us -> none  [the longest x1 4.52 us: lag_products(): return jnp.sum(skewed[:, :, :L], axis=1)]
  transfers between devices with their start and end apart: 2 -> 0, of which waited for: 1 -> 0; matrix products, arithmetic and copies ran while one was open for 3% -> 0% of each run, Pallas kernels for 0% -> 0%
where the time goes in v1:
time: 28 us; the launch traced here: 27.8 us
  Pallas kernels  26.5 us (95%)
  local copies, waits for them, and re-layouts  1.19 us (4%)
    pallas_call x1, Pallas kernels, body(): pl.pallas_call(functools.partial(kernel, sizes), out_shape=jax.ShapeDtype...  26.5 us
    unnamed x1, local copies, waits for them, and re-layouts  1.19 us

profile of v1, /device:TPU:1, one launch (start us, length us, event | category | flops | bytes accessed | tf_op | source)
XLA Modules:
  0.0 27.8 jit_solution(6241632416403632204)
XLA Ops:
  0.0 26.5 %shard_map.55 = f32[1,128]{1,0:T(1,128)} custom-call(f32[32,4096]{1,0:T(8,128)} %x_hbm.1, f32[32,4096]{1,0:T(8,128)} %y_hbm.1, bf16[768,768]{1,0:T(8,128)(2,1)} %constant.6.clone.fwd_hbm, bf16[2304,512]{1,0:T(8,128)(2,1)} %constant.7.clone.bwd_hbm, f32[8,384]{1,0:T(8,128)} %constant.8.clone.turns_hbm), custom_call_target="tpu_custom_call" | custom-call | tf_op jit(solution)/shard_map/pallas_call | solution.py:287
  26.6 1.2 %copy.7 = f32[1,128]{1,0:T(1,128)} copy(f32[1,128]{1,0:T(1,128)} %shard_map.55) | data formatting | bytes 1024

commit v2 on v0

v2 whole, which is shorter than its diff:
```python
import functools
import math

import jax
import jax.numpy as jnp
import ml_dtypes
import numpy as np
from jax import lax
from jax.experimental import pallas as pl
from jax.experimental.pallas import tpu as pltpu
from jax.sharding import PartitionSpec as P

L = 512
BLK = 128
N = 2 * BLK
MESH = pl.DeviceIdType.MESH


def halves(array):
    high = array.astype(ml_dtypes.bfloat16)
    low = (array - high.astype(np.float64)).astype(ml_dtypes.bfloat16)
    return high, low


@functools.cache
def tables():
    theta = 2 * np.pi * (np.arange(BLK) + 0.5) / N
    turns = np.outer(np.arange(BLK), theta)
    high, low = halves(np.concatenate([np.cos(turns), np.sin(turns)], axis=1))
    forward = np.stack([np.concatenate([high, high]), np.concatenate([low, low])])
    high, low = halves(np.concatenate([np.cos(turns.T), -np.sin(turns.T)]) * (2.0 / N))
    return forward, np.concatenate([high, low], axis=1)


def high_low(value):
    high = value.astype(jnp.bfloat16)
    return high, (value - high.astype(jnp.float32)).astype(jnp.bfloat16)


def kernel(
    sizes, x_hbm, y_hbm, fwd_hbm, bwd_hbm, out_ref,
    xv, yv, lead, head, fwd, bwd, parts, fx, fy, res, rparts, send, recv,
    load_sem, halo_sem, send_sem, recv_sem,
):
    zs, ys, xs = sizes
    pairs, length = xv.shape
    blocks, extra = length // BLK, L // BLK
    group = 2 * ys
    depth = zs // xs
    everyone = zs * group
    last = everyone - 1
    tm, mx = lax.axis_index("tm"), lax.axis_index("pair")
    mz, mg = tm // group, tm % group
    source_x = mz // depth
    own = jnp.where(source_x == mx, 1, 0)

    loads = [
        pltpu.make_async_copy(y_hbm.at[:, 0:L], lead, load_sem.at[0]),
        pltpu.make_async_copy(x_hbm, xv, load_sem.at[1]),
        pltpu.make_async_copy(fwd_hbm, fwd, load_sem.at[2]),
        pltpu.make_async_copy(y_hbm, yv, load_sem.at[3]),
        pltpu.make_async_copy(bwd_hbm, bwd, load_sem.at[4]),
    ]
    for load in loads:
        load.start()

    barrier = pltpu.get_barrier_semaphore()

    @pl.when(tm < last)
    def _():
        pl.semaphore_signal(barrier, inc=1, device_id=(tm + 1, mx), device_id_type=MESH)

    for step in range(1, everyone):
        other = lax.rem(tm + step, everyone)
        pl.semaphore_signal(barrier, inc=1, device_id=(other, source_x), device_id_type=MESH)

    @pl.when(own == 0)
    def _():
        pl.semaphore_signal(barrier, inc=1, device_id=(tm, source_x), device_id_type=MESH)

    def transform(value, at, into):
        count = value.shape[1] // BLK
        for j in range(count):
            high, low = high_low(value[:, j * BLK : (j + 1) * BLK])
            parts[j * pairs : (j + 1) * pairs, 0:BLK] = high
            parts[j * pairs : (j + 1) * pairs, BLK : 2 * BLK] = low
        rows = parts[0 : count * pairs, :]
        into[at * pairs : (at + count) * pairs, :] = jnp.dot(
            rows, fwd[0], preferred_element_type=jnp.float32
        ) + jnp.dot(rows, fwd[1], preferred_element_type=jnp.float32)

    loads[1].wait()
    loads[2].wait()
    transform(xv, 0, fx)

    loads[0].wait()
    pl.semaphore_wait(barrier, pairs * xs - own + jnp.where(tm > 0, 1, 0))
    halo = pltpu.make_async_remote_copy(
        src_ref=lead,
        dst_ref=head,
        send_sem=halo_sem.at[0],
        recv_sem=halo_sem.at[1],
        device_id=(jnp.maximum(tm - 1, 0), mx),
        device_id_type=MESH,
    )

    @pl.when(tm > 0)
    def _():
        halo.start()

    @pl.when(tm == last)
    def _():
        head[...] = jnp.zeros_like(head)

    loads[3].wait()
    transform(yv, 0, fy)

    lane = lax.broadcasted_iota(jnp.int32, (8, BLK), 1)
    sign = jnp.where(lane % 2 == 0, 1.0, -1.0).astype(jnp.float32)

    def take(ref, block, at):
        rows = pl.ds(pl.multiple_of(block * pairs + at, 8), 8)
        return ref[rows, 0:BLK], ref[rows, BLK : 2 * BLK]

    def products(at, first, past):
        sums = [None] * extra
        window = {}
        ahead = None
        for j in range(first, past):
            now = take(fy, j, at) if ahead is None else ahead
            ahead = take(fy, j + 1, at)
            window[j] = (now[0] - sign * ahead[1], now[1] + sign * ahead[0])
        terms = {}
        for q in range(extra):
            for b in range(blocks):
                if first <= b + q < past:
                    terms.setdefault(b, []).append(q)
        for b, lags in terms.items():
            cx, sx = take(fx, b, at)
            for q in lags:
                cz, sz = window[b + q]
                real, imag = cx * cz + sx * sz, sx * cz - cx * sz
                if sums[q] is not None:
                    real, imag = real + sums[q][0], imag + sums[q][1]
                sums[q] = (real, imag)
        return sums

    @pl.loop(0, pairs // 8)
    def _(g):
        at = pl.multiple_of(g * 8, 8)
        for q, (real, imag) in enumerate(products(at, 0, blocks - 1)):
            rows = pl.ds(pl.multiple_of(q * pairs + at, 8), 8)
            res[rows, 0:BLK] = real
            res[rows, BLK : 2 * BLK] = imag

    @pl.when(tm < last)
    def _():
        halo.wait_recv()

    transform(head, blocks, fy)
    for at in range(0, pairs, 8):
        for q, (real, imag) in enumerate(products(at, blocks - 1, blocks + extra - 1)):
            rows = slice(q * pairs + at, q * pairs + at + 8)
            for half, value in enumerate((real, imag)):
                columns = slice(half * BLK, (half + 1) * BLK)
                high, low = high_low(res[rows, columns] + value)
                rparts[rows, columns] = high.astype(jnp.float32)
                rparts[extra * pairs + q * pairs + at : extra * pairs + q * pairs + at + 8, columns] = low.astype(jnp.float32)

    loads[4].wait()
    both = jnp.dot(rparts[...].astype(jnp.bfloat16), bwd[...], preferred_element_type=jnp.float32)
    half = extra * pairs
    lagged = (both[0:half, 0:BLK] + both[0:half, BLK : 2 * BLK]) + (
        both[half:, 0:BLK] + both[half:, BLK : 2 * BLK]
    )
    send[...] = lagged.reshape(half, 1, BLK)

    def copy(row, q):
        return pltpu.make_async_remote_copy(
            src_ref=send.at[q * pairs + row],
            dst_ref=recv.at[tm],
            send_sem=send_sem,
            recv_sem=recv_sem,
            device_id=(mx * pairs + row, q),
            device_id_type=MESH,
        )

    order = [0]
    for d in range(1, ys // 2):
        order += [d, ys - d]
    order.append(ys // 2)
    for y in order:
        for e in range(depth):
            for c in (0, 1):
                row = e * group + y * 2 + c
                for step in range(1, xs):
                    copy(row, lax.rem(mx + step, xs)).start()

                @pl.when(mx * pairs + row != tm)
                def _():
                    copy(row, mx).start()

    @pl.when(own == 1)
    def _():
        recv[tm] = send[mx * pairs + (tm - mx * pairs)]

    def all_of(count):
        return pltpu.make_async_remote_copy(
            src_ref=send.at[pl.ds(0, count)],
            dst_ref=recv.at[pl.ds(0, count)],
            send_sem=send_sem,
            recv_sem=recv_sem,
            device_id=(tm, mx),
            device_id_type=MESH,
        )

    for own_too in (0, 1):

        @pl.when(own == own_too)
        def _():
            all_of(everyone - own_too).wait_recv()

    sums = [recv[i] for i in range(8)]
    for i in range(8, everyone):
        sums[i % 8] = sums[i % 8] + recv[i]
    while len(sums) > 1:
        sums = [a + b for a, b in zip(sums[0::2], sums[1::2])]
    out_ref[...] = sums[0]

    @pl.when(tm > 0)
    def _():
        halo.wait_send()

    for own_too in (0, 1):

        @pl.when(own == own_too)
        def _():
            all_of(everyone - own_too).wait_send()


def body(sizes, total, x_series, y_series):
    fwd, bwd = tables()
    zs, ys, xs = sizes
    pairs, length = x_series.shape
    blocks, extra = length // BLK, L // BLK
    f32, bf16 = jnp.float32, jnp.bfloat16
    dma = pltpu.SemaphoreType.DMA
    lagged = pl.pallas_call(
        functools.partial(kernel, sizes),
        out_shape=jax.ShapeDtypeStruct((1, L // xs), f32),
        in_specs=[pl.BlockSpec(memory_space=pl.ANY)] * 4,
        out_specs=pl.BlockSpec(memory_space=pltpu.VMEM),
        scratch_shapes=[
            pltpu.VMEM((pairs, length), f32),
            pltpu.VMEM((pairs, length), f32),
            pltpu.VMEM((pairs, L), f32),
            pltpu.VMEM((pairs, L), f32),
            pltpu.VMEM(fwd.shape, bf16),
            pltpu.VMEM(bwd.shape, bf16),
            pltpu.VMEM((blocks * pairs, 2 * BLK), bf16),
            pltpu.VMEM((blocks * pairs, N), f32),
            pltpu.VMEM(((blocks + extra) * pairs, N), f32),
            pltpu.VMEM((extra * pairs, N), f32),
            pltpu.VMEM((2 * extra * pairs, N), f32),
            pltpu.VMEM((pairs * xs, 1, L // xs), f32),
            pltpu.VMEM((2 * zs * ys, 1, L // xs), f32),
            dma((5,)),
            dma((2,)),
            dma,
            dma,
        ],
        compiler_params=pltpu.CompilerParams(collective_id=0, has_side_effects=True),
    )(x_series, y_series, jnp.asarray(fwd), jnp.asarray(bwd))
    return lagged * (1.0 / math.sqrt(total))


def solution(mesh):
    sizes = (8, 8, mesh.shape["pair"])
    total = 524288
    return jax.shard_map(
        functools.partial(body, sizes, total),
        mesh=mesh,
        in_specs=(P("pair", "tm"), P("pair", "tm")),
        out_specs=P("tm", "pair"),
        check_vma=False,
    )
```

time: 130 us -> 25.8 us (0.20)
  blocking collectives: 46.1 us -> 0 us
  local copies, waits for them, and re-layouts: 41.4 us -> 0 us
  Pallas kernels: 0 us -> 24.5 us
  matrix products: 19 us -> 0 us
  starting transfers between devices: 12.7 us -> 0 us
  waiting for transfers between devices: 4.48 us -> 0 us
  other arithmetic: 5.13 us -> 1.19 us
    all_to_all x4 -> x0, blocking collectives: 46.1 us -> none  [the longest x1 21.6 us: sum_by_axis(): return jnp.sum(lax.all_to_all(own, far, 0, 0, tiled=True), axis=0)]
    pallas_call x0 -> x1, Pallas kernels: none -> 24.5 us  [body(): pl.pallas_call(functools.partial(kernel, sizes), out_shape=jax.ShapeDtype...]
    dot_general x1 -> x0, matrix products: 19 us -> none  [lag_products(): jnp.einsum('pbi,pbj->pij', left_rows, right_rows, precision=lax.Precision...]
    unnamed x13 -> x0, local copies, waits for them, and re-layouts: 16.2 us -> none
    reshape x1 -> x0, local copies, waits for them, and re-layouts: 14.9 us -> none  [lag_products(): skewed = flattened.reshape(pair_count, block_len, span_cols + 1)]
    ppermute x1 -> x0, starting transfers between devices: 8.73 us -> none  [passed_along(): return lax.ppermute(array, axis, pairs)]
    pad x1 -> x0, local copies, waits for them, and re-layouts: 8.56 us -> none  [lag_products(): flattened = jnp.pad(flattened, ((0, 0), (0, block_len)))]
    reduce_sum x3 -> x0, other arithmetic: 4.61 us -> none  [the longest x1 4.52 us: lag_products(): return jnp.sum(skewed[:, :, :L], axis=1)]
  transfers between devices with their start and end apart: 2 -> 0, of which waited for: 1 -> 0; matrix products, arithmetic and copies ran while one was open for 3% -> 0% of each run, Pallas kernels for 0% -> 0%
where the time goes in v2:
time: 25.8 us; the launch traced here: 25.7 us
  Pallas kernels  24.5 us (95%)
  other arithmetic  1.19 us (5%)
    pallas_call x1, Pallas kernels, body(): pl.pallas_call(functools.partial(kernel, sizes), out_shape=jax.ShapeDtype...  24.5 us
    mul x1, other arithmetic, body(): return lagged * (1.0 / math.sqrt(total))  1.19 us

profile of v2, /device:TPU:1, one launch (start us, length us, event | category | flops | bytes accessed | tf_op | source)
XLA Modules:
  0.0 25.7 jit_solution(12157450336770930257)
XLA Ops:
  0.0 24.5 %shard_map.46 = f32[1,128]{1,0:T(1,128)} custom-call(f32[32,4096]{1,0:T(8,128)} %x_hbm.1, f32[32,4096]{1,0:T(8,128)} %y_hbm.1, bf16[2,256,256]{2,1,0:T(8,128)(2,1)} %constant.6.clone.fwd_hbm, bf16[256,256]{1,0:T(8,128)(2,1)} %constant.7.clone.bwd_hbm), custom_call_target="tpu_custom_call" | custom-call | tf_op jit(solution)/shard_map/pallas_call | solution.py:248
  24.5 1.2 %broadcast_multiply_fusion = f32[1,128]{1,0:T(1,128)} fusion(f32[1,128]{1,0:T(1,128)} %shard_map.46), kind=kLoop, calls=%fused_computation | loop fusion | flops 128 | bytes 1024 | tf_op jit(solution)/shard_map/mul | solution.py:274

commit v3 on v2

--- a/solution.py
+++ b/solution.py
@@ -23,12 +23,12 @@
 
 
 @functools.cache
-def tables():
+def tables(total):
     theta = 2 * np.pi * (np.arange(BLK) + 0.5) / N
     turns = np.outer(np.arange(BLK), theta)
     high, low = halves(np.concatenate([np.cos(turns), np.sin(turns)], axis=1))
     forward = np.stack([np.concatenate([high, high]), np.concatenate([low, low])])
-    high, low = halves(np.concatenate([np.cos(turns.T), -np.sin(turns.T)]) * (2.0 / N))
+    high, low = halves(np.concatenate([np.cos(turns.T), -np.sin(turns.T)]) * (2.0 / N / math.sqrt(total)))
     return forward, np.concatenate([high, low], axis=1)
 
 
@@ -38,8 +38,8 @@
 
 
 def kernel(
-    sizes, x_hbm, y_hbm, fwd_hbm, bwd_hbm, out_ref,
-    xv, yv, lead, head, fwd, bwd, parts, fx, fy, res, rparts, send, recv,
+    sizes, x_hbm, y_hbm, fwd_hbm, bwd_hbm, recv,
+    xv, yv, lead, head, fwd, bwd, parts, fx, fy, res, rparts, send,
     load_sem, halo_sem, send_sem, recv_sem,
 ):
     zs, ys, xs = sizes
@@ -89,10 +89,6 @@
             rows, fwd[0], preferred_element_type=jnp.float32
         ) + jnp.dot(rows, fwd[1], preferred_element_type=jnp.float32)
 
-    loads[1].wait()
-    loads[2].wait()
-    transform(xv, 0, fx)
-
     loads[0].wait()
     pl.semaphore_wait(barrier, pairs * xs - own + jnp.where(tm > 0, 1, 0))
     halo = pltpu.make_async_remote_copy(
@@ -111,6 +107,10 @@
     @pl.when(tm == last)
     def _():
         head[...] = jnp.zeros_like(head)
+
+    loads[1].wait()
+    loads[2].wait()
+    transform(xv, 0, fx)
 
     loads[3].wait()
     transform(yv, 0, fy)
@@ -200,9 +200,11 @@
                 def _():
                     copy(row, mx).start()
 
+    kept = pltpu.make_async_copy(send.at[tm], recv.at[tm], load_sem.at[5])
+
     @pl.when(own == 1)
     def _():
-        recv[tm] = send[mx * pairs + (tm - mx * pairs)]
+        kept.start()
 
     def all_of(count):
         return pltpu.make_async_remote_copy(
@@ -220,12 +222,9 @@
         def _():
             all_of(everyone - own_too).wait_recv()
 
-    sums = [recv[i] for i in range(8)]
-    for i in range(8, everyone):
-        sums[i % 8] = sums[i % 8] + recv[i]
-    while len(sums) > 1:
-        sums = [a + b for a, b in zip(sums[0::2], sums[1::2])]
-    out_ref[...] = sums[0]
+    @pl.when(own == 1)
+    def _():
+        kept.wait()
 
     @pl.when(tm > 0)
     def _():
@@ -239,17 +238,17 @@
 
 
 def body(sizes, total, x_series, y_series):
-    fwd, bwd = tables()
+    fwd, bwd = tables(total)
     zs, ys, xs = sizes
     pairs, length = x_series.shape
     blocks, extra = length // BLK, L // BLK
     f32, bf16 = jnp.float32, jnp.bfloat16
     dma = pltpu.SemaphoreType.DMA
-    lagged = pl.pallas_call(
+    shares = pl.pallas_call(
         functools.partial(kernel, sizes),
-        out_shape=jax.ShapeDtypeStruct((1, L // xs), f32),
+        out_shape=pltpu.VMEM((2 * zs * ys, 1, L // xs), f32),
         in_specs=[pl.BlockSpec(memory_space=pl.ANY)] * 4,
-        out_specs=pl.BlockSpec(memory_space=pltpu.VMEM),
+        out_specs=pl.BlockSpec(memory_space=pl.ANY),
         scratch_shapes=[
             pltpu.VMEM((pairs, length), f32),
             pltpu.VMEM((pairs, length), f32),
@@ -263,15 +262,14 @@
             pltpu.VMEM((extra * pairs, N), f32),
             pltpu.VMEM((2 * extra * pairs, N), f32),
             pltpu.VMEM((pairs * xs, 1, L // xs), f32),
-            pltpu.VMEM((2 * zs * ys, 1, L // xs), f32),
-            dma((5,)),
+            dma((6,)),
             dma((2,)),
             dma,
             dma,
         ],
         compiler_params=pltpu.CompilerParams(collective_id=0, has_side_effects=True),
     )(x_series, y_series, jnp.asarray(fwd), jnp.asarray(bwd))
-    return lagged * (1.0 / math.sqrt(total))
+    return jnp.sum(shares, axis=0)
 
 
 def solution(mesh):

time: 25.8 us -> 24.6 us (0.953)
  Pallas kernels: 24.5 us -> 23.8 us
  other arithmetic: 1.19 us -> 0.66 us
    mul x1 -> x0, other arithmetic: 1.19 us -> none  [body(): return lagged * (1.0 / math.sqrt(total))]
    pallas_call x1, Pallas kernels: 24.5 us -> 23.8 us  [body(): pl.pallas_call(functools.partial(kernel, sizes), out_shape=pltpu.VMEM((2...]
    reduce_sum x0 -> x1, other arithmetic: none -> 0.66 us  [body(): return jnp.sum(shares, axis=0)]
where the time goes in v3:
time: 24.6 us; the launch traced here: 24.5 us
  Pallas kernels  23.8 us (97%)
  other arithmetic  0.66 us (3%)
    pallas_call x1, Pallas kernels, body(): pl.pallas_call(functools.partial(kernel, sizes), out_shape=pltpu.VMEM((2...  23.8 us
    reduce_sum x1, other arithmetic, body(): return jnp.sum(shares, axis=0)  0.66 us

profile of v3, /device:TPU:1, one launch (start us, length us, event | category | flops | bytes accessed | tf_op | source)
XLA Modules:
  0.0 24.5 jit_solution(13546472898302081308)
XLA Ops:
  0.0 23.8 %shard_map.46 = f32[128,1,128]{2,1,0:T(1,128)S(1)} custom-call(f32[32,4096]{1,0:T(8,128)} %x_hbm.1, f32[32,4096]{1,0:T(8,128)} %y_hbm.1, bf16[2,256,256]{2,1,0:T(8,128)(2,1)} %constant.6.clone.fwd_hbm, bf16[256,256]{1,0:T(8,128)(2,1)} %constant.7.clone.bwd_hbm), custom_call_target="tpu_custom_call" | custom-call | tf_op jit(solution)/shard_map/pallas_call | solution.py:247
  23.8 0.7 %reduce_sum.11 = f32[128]{0:T(128)} reduce(f32[128,1,128]{2,1,0:T(1,128)S(1)} %shard_map.46, f32[]{:T(128)} %constant.2.clone.1), dimensions={0,1}, to_apply=%region_0.0 | reduce | flops 16256 | bytes 66052 | tf_op jit(solution)/shard_map/reduce_sum | solution.py:272

commit v4 on v3

v4 whole, which is shorter than its diff:
```python
import functools
import math

import jax
import jax.numpy as jnp
import ml_dtypes
import numpy as np
from jax import lax
from jax.experimental import pallas as pl
from jax.experimental.pallas import tpu as pltpu
from jax.sharding import PartitionSpec as P

L = 512
BLK = 128
N = 2 * BLK
MESH = pl.DeviceIdType.MESH


def halves(array):
    high = array.astype(ml_dtypes.bfloat16)
    low = (array - high.astype(np.float64)).astype(ml_dtypes.bfloat16)
    return high, low


@functools.cache
def tables(total):
    theta = 2 * np.pi * (np.arange(BLK) + 0.5) / N
    turns = np.outer(np.arange(BLK), theta)
    high, low = halves(np.concatenate([np.cos(turns), np.sin(turns)], axis=1))
    forward = np.stack([np.concatenate([high, high]), np.concatenate([low, low])])
    high, low = halves(np.concatenate([np.cos(turns.T), -np.sin(turns.T)]) * (2.0 / N / math.sqrt(total)))
    return forward, np.concatenate([high, low], axis=1)


def high_low(value):
    high = value.astype(jnp.bfloat16)
    return high, (value - high.astype(jnp.float32)).astype(jnp.bfloat16)


def kernel(
    sizes, x_hbm, y_hbm, fwd_hbm, bwd_hbm, recv,
    xv, yv, edges, halo, fwd, bwd, parts, fx, fy, fh, res, rparts, send,
    load_sem, halo_sem, send_sem, recv_sem,
):
    zs, ys, xs = sizes
    pairs, length = xv.shape
    blocks, extra = length // BLK, L // BLK
    near = extra // 2
    reach = near * BLK
    group = 2 * ys
    depth = zs // xs
    everyone = zs * group
    last = everyone - 1
    tm, mx = lax.axis_index("tm"), lax.axis_index("pair")
    mz, mg = tm // group, tm % group
    source_x = mz // depth
    own = jnp.where(source_x == mx, 1, 0)

    loads = [
        pltpu.make_async_copy(y_hbm.at[:, 0:reach], edges.at[0], load_sem.at[0]),
        pltpu.make_async_copy(x_hbm.at[:, length - reach : length], edges.at[1], load_sem.at[6]),
        pltpu.make_async_copy(x_hbm, xv, load_sem.at[1]),
        pltpu.make_async_copy(fwd_hbm, fwd, load_sem.at[2]),
        pltpu.make_async_copy(y_hbm, yv, load_sem.at[3]),
        pltpu.make_async_copy(bwd_hbm, bwd, load_sem.at[4]),
    ]
    for load in loads:
        load.start()

    barrier = pltpu.get_barrier_semaphore()

    for step, there in ((1, tm < last), (-1, tm > 0)):

        @pl.when(there)
        def _():
            pl.semaphore_signal(barrier, inc=1, device_id=(tm + step, mx), device_id_type=MESH)

    for other in range(everyone):

        @pl.when(jnp.logical_or(source_x != mx, tm != other))
        def _():
            pl.semaphore_signal(barrier, inc=1, device_id=(other, source_x), device_id_type=MESH)

    def transform(values, into):
        count = 0
        for value in values:
            for j in range(value.shape[1] // BLK):
                high, low = high_low(value[:, j * BLK : (j + 1) * BLK])
                parts[count * pairs : (count + 1) * pairs, 0:BLK] = high
                parts[count * pairs : (count + 1) * pairs, BLK : 2 * BLK] = low
                count += 1
        rows = parts[0 : count * pairs, :]
        into[...] = jnp.dot(rows, fwd[0], preferred_element_type=jnp.float32) + jnp.dot(
            rows, fwd[1], preferred_element_type=jnp.float32
        )

    loads[0].wait()
    loads[1].wait()
    neighbours = jnp.where(tm > 0, 1, 0) + jnp.where(tm < last, 1, 0)
    pl.semaphore_wait(barrier, pairs * xs - own + neighbours)

    def swap(side, other):
        return pltpu.make_async_remote_copy(
            src_ref=edges.at[side],
            dst_ref=halo.at[side],
            send_sem=halo_sem.at[side],
            recv_sem=halo_sem.at[2 + side],
            device_id=(other, mx),
            device_id_type=MESH,
        )

    to_before, to_next = swap(0, jnp.maximum(tm - 1, 0)), swap(1, jnp.minimum(tm + 1, last))

    @pl.when(tm > 0)
    def _():
        to_before.start()

    @pl.when(tm < last)
    def _():
        to_next.start()

    @pl.when(tm == last)
    def _():
        halo[0] = jnp.zeros((pairs, reach), jnp.float32)

    @pl.when(tm == 0)
    def _():
        halo[1] = jnp.zeros((pairs, reach), jnp.float32)

    loads[2].wait()
    loads[3].wait()
    transform([xv], fx)

    loads[4].wait()
    transform([yv], fy)

    lane = lax.broadcasted_iota(jnp.int32, (8, BLK), 1)
    sign = jnp.where(lane % 2 == 0, 1.0, -1.0).astype(jnp.float32)

    def take(ref, block, at):
        rows = pl.ds(pl.multiple_of(block * pairs + at, 8), 8)
        return ref[rows, 0:BLK], ref[rows, BLK : 2 * BLK]

    def turned(value):
        return -sign * value[1], sign * value[0]

    def plus(a, b):
        return b if a is None else (a[0] + b[0], a[1] + b[1])

    def add(sums, q, a, b):
        (ca, sa), (cb, sb) = a, b
        sums[q] = plus(sums[q], (ca * cb + sa * sb, sa * cb - ca * sb))

    def inner(at):
        window = {}
        now = take(fy, 0, at)
        for j in range(blocks - 1):
            ahead = take(fy, j + 1, at)
            window[j] = plus(now, turned(ahead))
            now = ahead
        sums = [None] * extra
        for b in range(blocks - 1):
            x = take(fx, b, at)
            for q in range(extra):
                if b + q < blocks - 1:
                    add(sums, q, x, window[b + q])
        return sums

    def outer(at):
        y = [take(fh, j, at) for j in range(near)]
        window = [plus(take(fy, blocks - 1, at), turned(y[0]))]
        window += [plus(y[j], turned(y[j + 1])) for j in range(near - 1)] + [y[near - 1]]
        sums = [None] * extra
        for b in range(blocks - extra, blocks):
            x = take(fx, b, at)
            for q in range(extra):
                if 0 <= b + q - (blocks - 1) <= near:
                    add(sums, q, x, window[b + q - (blocks - 1)])
        for b in range(near):
            x = take(fh, near + b, at)
            for q in range(extra):
                j = b - near + q
                if j >= near:
                    add(sums, q, x, plus(take(fy, j, at), turned(take(fy, j + 1, at))))
                elif j == near - 1:
                    add(sums, q, x, turned(take(fy, near, at)))
        return sums

    @pl.loop(0, pairs // 8)
    def _(g):
        at = pl.multiple_of(g * 8, 8)
        for q, (real, imag) in enumerate(inner(at)):
            rows = pl.ds(pl.multiple_of(q * pairs + at, 8), 8)
            res[rows, 0:BLK] = real
            res[rows, BLK : 2 * BLK] = imag

    @pl.when(tm < last)
    def _():
        to_before.wait_recv()

    @pl.when(tm > 0)
    def _():
        to_next.wait_recv()

    transform([halo.at[0], halo.at[1]], fh)
    for at in range(0, pairs, 8):
        for q, (real, imag) in enumerate(outer(at)):
            rows = slice(q * pairs + at, q * pairs + at + 8)
            for half, value in enumerate((real, imag)):
                columns = slice(half * BLK, (half + 1) * BLK)
                high, low = high_low(res[rows, columns] + value)
                rparts[rows, columns] = high.astype(jnp.float32)
                rparts[extra * pairs + q * pairs + at : extra * pairs + q * pairs + at + 8, columns] = low.astype(jnp.float32)

    loads[5].wait()
    both = jnp.dot(rparts[...].astype(jnp.bfloat16), bwd[...], preferred_element_type=jnp.float32)
    half = extra * pairs
    lagged = (both[0:half, 0:BLK] + both[0:half, BLK : 2 * BLK]) + (
        both[half:, 0:BLK] + both[half:, BLK : 2 * BLK]
    )
    send[...] = lagged.reshape(half, 1, BLK)

    def copy(row, q):
        return pltpu.make_async_remote_copy(
            src_ref=send.at[q * pairs + row],
            dst_ref=recv.at[tm],
            send_sem=send_sem,
            recv_sem=recv_sem,
            device_id=(mx * pairs + row, q),
            device_id_type=MESH,
        )

    own_at = jnp.where(own == 1, tm, -1)
    order = [0]
    for d in range(1, ys // 2):
        order += [d, ys - d]
    order.append(ys // 2)
    for y in order:
        for e in range(depth):
            for c in (0, 1):
                row = e * group + y * 2 + c
                for q in range(xs):

                    @pl.when(own_at != q * pairs + row)
                    def _():
                        copy(row, q).start()

    kept = pltpu.make_async_copy(send.at[tm], recv.at[tm], load_sem.at[5])

    @pl.when(own == 1)
    def _():
        kept.start()

    def all_of(count):
        return pltpu.make_async_remote_copy(
            src_ref=send.at[pl.ds(0, count)],
            dst_ref=recv.at[pl.ds(0, count)],
            send_sem=send_sem,
            recv_sem=recv_sem,
            device_id=(tm, mx),
            device_id_type=MESH,
        )

    for own_too in (0, 1):

        @pl.when(own == own_too)
        def _():
            all_of(everyone - own_too).wait_recv()

    @pl.when(own == 1)
    def _():
        kept.wait()

    @pl.when(tm > 0)
    def _():
        to_before.wait_send()

    @pl.when(tm < last)
    def _():
        to_next.wait_send()

    for own_too in (0, 1):

        @pl.when(own == own_too)
        def _():
            all_of(everyone - own_too).wait_send()


def body(sizes, total, x_series, y_series):
    fwd, bwd = tables(total)
    zs, ys, xs = sizes
    pairs, length = x_series.shape
    blocks, extra = length // BLK, L // BLK
    f32, bf16 = jnp.float32, jnp.bfloat16
    dma = pltpu.SemaphoreType.DMA
    shares = pl.pallas_call(
        functools.partial(kernel, sizes),
        out_shape=pltpu.VMEM((2 * zs * ys, 1, L // xs), f32),
        in_specs=[pl.BlockSpec(memory_space=pl.ANY)] * 4,
        out_specs=pl.BlockSpec(memory_space=pl.ANY),
        scratch_shapes=[
            pltpu.VMEM((pairs, length), f32),
            pltpu.VMEM((pairs, length), f32),
            pltpu.VMEM((2, pairs, L // 2), f32),
            pltpu.VMEM((2, pairs, L // 2), f32),
            pltpu.VMEM(fwd.shape, bf16),
            pltpu.VMEM(bwd.shape, bf16),
            pltpu.VMEM((blocks * pairs, 2 * BLK), bf16),
            pltpu.VMEM((blocks * pairs, N), f32),
            pltpu.VMEM((blocks * pairs, N), f32),
            pltpu.VMEM((extra * pairs, N), f32),
            pltpu.VMEM((extra * pairs, N), f32),
            pltpu.VMEM((2 * extra * pairs, N), f32),
            pltpu.VMEM((pairs * xs, 1, L // xs), f32),
            dma((7,)),
            dma((4,)),
            dma,
            dma,
        ],
        compiler_params=pltpu.CompilerParams(collective_id=0, has_side_effects=True),
    )(x_series, y_series, jnp.asarray(fwd), jnp.asarray(bwd))
    return jnp.sum(shares, axis=0)


def solution(mesh):
    sizes = (8, 8, mesh.shape["pair"])
    total = 524288
    return jax.shard_map(
        functools.partial(body, sizes, total),
        mesh=mesh,
        in_specs=(P("pair", "tm"), P("pair", "tm")),
        out_specs=P("tm", "pair"),
        check_vma=False,
    )
```

time: 24.6 us -> 24.6 us (level)
  no operation moved by 1% of the time
where the time goes in v4:
time: 24.6 us; the launch traced here: 24.5 us
  Pallas kernels  23.8 us (97%)
  other arithmetic  0.66 us (3%)
    pallas_call x1, Pallas kernels, body(): pl.pallas_call(functools.partial(kernel, sizes), out_shape=pltpu.VMEM((2...  23.8 us
    reduce_sum x1, other arithmetic, body(): return jnp.sum(shares, axis=0)  0.66 us

profile of v4, /device:TPU:1, one launch (start us, length us, event | category | flops | bytes accessed | tf_op | source)
XLA Modules:
  0.0 24.5 jit_solution(10522268634448979776)
XLA Ops:
  0.0 23.8 %shard_map.46 = f32[128,1,128]{2,1,0:T(1,128)S(1)} custom-call(f32[32,4096]{1,0:T(8,128)} %x_hbm.1, f32[32,4096]{1,0:T(8,128)} %y_hbm.1, bf16[2,256,256]{2,1,0:T(8,128)(2,1)} %constant.6.clone.fwd_hbm, bf16[256,256]{1,0:T(8,128)(2,1)} %constant.7.clone.bwd_hbm), custom_call_target="tpu_custom_call" | custom-call | tf_op jit(solution)/shard_map/pallas_call | solution.py:296
  23.9 0.7 %reduce_sum.11 = f32[128]{0:T(128)} reduce(f32[128,1,128]{2,1,0:T(1,128)S(1)} %shard_map.46, f32[]{:T(128)} %constant.2.clone.1), dimensions={0,1}, to_apply=%region_0.0 | reduce | flops 16256 | bytes 66052 | tf_op jit(solution)/shard_map/reduce_sum | solution.py:322

commit v5 on v4

--- a/solution.py
+++ b/solution.py
@@ -30,6 +30,10 @@
     forward = np.stack([np.concatenate([high, high]), np.concatenate([low, low])])
     high, low = halves(np.concatenate([np.cos(turns.T), -np.sin(turns.T)]) * (2.0 / N / math.sqrt(total)))
     return forward, np.concatenate([high, low], axis=1)
+
+
+def from_far(count):
+    return sorted(range(1, count), key=lambda d: -min(d, count - d))
 
 
 def high_low(value):
@@ -75,11 +79,21 @@
         def _():
             pl.semaphore_signal(barrier, inc=1, device_id=(tm + step, mx), device_id_type=MESH)
 
-    for other in range(everyone):
-
-        @pl.when(jnp.logical_or(source_x != mx, tm != other))
-        def _():
-            pl.semaphore_signal(barrier, inc=1, device_id=(other, source_x), device_id_type=MESH)
+    def here(z, g):
+        pl.semaphore_signal(
+            barrier, inc=1, device_id=(z * group + g, source_x), device_id_type=MESH
+        )
+
+    for d in from_far(zs):
+        z = lax.rem(mz + d, zs)
+        for g in range(group):
+            here(z, g)
+    for d in range(1, group):
+        here(mz, lax.rem(mg + d, group))
+
+    @pl.when(own == 0)
+    def _():
+        here(mz, mg)
 
     def transform(values, into):
         count = 0
@@ -231,13 +245,9 @@
         )
 
     own_at = jnp.where(own == 1, tm, -1)
-    order = [0]
-    for d in range(1, ys // 2):
-        order += [d, ys - d]
-    order.append(ys // 2)
-    for y in order:
-        for e in range(depth):
-            for c in (0, 1):
+    for e in range(depth):
+        for y in range(ys):
+            for c in (1, 0):
                 row = e * group + y * 2 + c
                 for q in range(xs):
 

time: 24.6 us -> 24 us (0.976)
  Pallas kernels: 23.8 us -> 23.3 us
    pallas_call x1, Pallas kernels: 23.8 us -> 23.3 us  [body(): pl.pallas_call(functools.partial(kernel, sizes), out_shape=pltpu.VMEM((2...]
where the time goes in v5:
time: 24 us; the launch traced here: 23.9 us
  Pallas kernels  23.3 us (97%)
  other arithmetic  0.66 us (3%)
    pallas_call x1, Pallas kernels, body(): pl.pallas_call(functools.partial(kernel, sizes), out_shape=pltpu.VMEM((2...  23.3 us
    reduce_sum x1, other arithmetic, body(): return jnp.sum(shares, axis=0)  0.66 us

profile of v5, /device:TPU:1, one launch (start us, length us, event | category | flops | bytes accessed | tf_op | source)
XLA Modules:
  0.0 23.9 jit_solution(17736459341758600394)
XLA Ops:
  0.0 23.3 %shard_map.46 = f32[128,1,128]{2,1,0:T(1,128)S(1)} custom-call(f32[32,4096]{1,0:T(8,128)} %x_hbm.1, f32[32,4096]{1,0:T(8,128)} %y_hbm.1, bf16[2,256,256]{2,1,0:T(8,128)(2,1)} %constant.6.clone.fwd_hbm, bf16[256,256]{1,0:T(8,128)(2,1)} %constant.7.clone.bwd_hbm), custom_call_target="tpu_custom_call" | custom-call | tf_op jit(solution)/shard_map/pallas_call | solution.py:306
  23.3 0.7 %reduce_sum.11 = f32[128]{0:T(128)} reduce(f32[128,1,128]{2,1,0:T(1,128)S(1)} %shard_map.46, f32[]{:T(128)} %constant.2.clone.1), dimensions={0,1}, to_apply=%region_0.0 | reduce | flops 16256 | bytes 66052 | tf_op jit(solution)/shard_map/reduce_sum | solution.py:332

commit v6 on v5

--- a/solution.py
+++ b/solution.py
@@ -43,20 +43,24 @@
 
 def kernel(
     sizes, x_hbm, y_hbm, fwd_hbm, bwd_hbm, recv,
-    xv, yv, edges, halo, fwd, bwd, parts, fx, fy, fh, res, rparts, send,
-    load_sem, halo_sem, send_sem, recv_sem,
+    xv, yv, edges, halo, fwd, bwd,
+    px0, px1, py0, py1, ph0, ph1, fx0, fx1, fy0, fy1, fh0, fh1, res, rparts, send,
+    load_sem, halo_sem, send_sem, recv_sem, told,
 ):
     zs, ys, xs = sizes
     pairs, length = xv.shape
     blocks, extra = length // BLK, L // BLK
     near = extra // 2
     reach = near * BLK
+    half = pairs // 2
+    first, second = slice(0, half), slice(half, pairs)
     group = 2 * ys
     depth = zs // xs
     everyone = zs * group
     last = everyone - 1
     tm, mx = lax.axis_index("tm"), lax.axis_index("pair")
     mz, mg = tm // group, tm % group
+    my, mc = mg // 2, mg % 2
     source_x = mz // depth
     own = jnp.where(source_x == mx, 1, 0)
 
@@ -73,45 +77,44 @@
 
     barrier = pltpu.get_barrier_semaphore()
 
-    for step, there in ((1, tm < last), (-1, tm > 0)):
-
-        @pl.when(there)
+    def arrived(device, x):
+        pl.semaphore_signal(barrier, inc=1, device_id=(device, x), device_id_type=MESH)
+
+    def tell(which, device):
+        pl.semaphore_signal(told.at[which], inc=1, device_id=(device, mx), device_id_type=MESH)
+
+    @pl.when(mc == 1)
+    def _():
+        arrived(tm - 1, mx)
+
+    @pl.when(jnp.logical_and(mc == 1, tm < last))
+    def _():
+        arrived(tm + 1, mx)
+
+    def greet():
+        for d in from_far(zs):
+            z = lax.rem(mz + d, zs)
+            for y in range(ys):
+                arrived(z * group + 2 * y + 1, source_x)
+        for d in range(1, ys):
+            arrived(mz * group + 2 * lax.rem(my + d, ys) + 1, source_x)
+
+        @pl.when(jnp.logical_or(own == 0, mc == 0))
         def _():
-            pl.semaphore_signal(barrier, inc=1, device_id=(tm + step, mx), device_id_type=MESH)
-
-    def here(z, g):
-        pl.semaphore_signal(
-            barrier, inc=1, device_id=(z * group + g, source_x), device_id_type=MESH
-        )
-
-    for d in from_far(zs):
-        z = lax.rem(mz + d, zs)
-        for g in range(group):
-            here(z, g)
-    for d in range(1, group):
-        here(mz, lax.rem(mg + d, group))
-
-    @pl.when(own == 0)
-    def _():
-        here(mz, mg)
-
-    def transform(values, into):
+            arrived(mz * group + 2 * my + 1, source_x)
+
+    def transform(values, part, into):
         count = 0
         for value in values:
             for j in range(value.shape[1] // BLK):
                 high, low = high_low(value[:, j * BLK : (j + 1) * BLK])
-                parts[count * pairs : (count + 1) * pairs, 0:BLK] = high
-                parts[count * pairs : (count + 1) * pairs, BLK : 2 * BLK] = low
+                part[count * half : (count + 1) * half, 0:BLK] = high
+                part[count * half : (count + 1) * half, BLK : 2 * BLK] = low
                 count += 1
-        rows = parts[0 : count * pairs, :]
+        rows = part[0 : count * half, :]
         into[...] = jnp.dot(rows, fwd[0], preferred_element_type=jnp.float32) + jnp.dot(
             rows, fwd[1], preferred_element_type=jnp.float32
         )
-
-    loads[0].wait()
-    loads[1].wait()
-    neighbours = jnp.where(tm > 0, 1, 0) + jnp.where(tm < last, 1, 0)
-    pl.semaphore_wait(barrier, pairs * xs - own + neighbours)
 
     def swap(side, other):
         return pltpu.make_async_remote_copy(
@@ -125,13 +128,31 @@
 
     to_before, to_next = swap(0, jnp.maximum(tm - 1, 0)), swap(1, jnp.minimum(tm + 1, last))
 
+    @pl.when(mc == 0)
+    def _():
+        pl.semaphore_wait(barrier, 1 + jnp.where(tm > 0, 1, 0))
+        tell(0, tm + 1)
+
+    @pl.when(jnp.logical_and(mc == 0, tm > 0))
+    def _():
+        tell(1, tm - 1)
+
+    @pl.when(mc == 1)
+    def _():
+        greet()
+        pl.semaphore_wait(told.at[0], 1)
+
+    loads[0].wait()
+
     @pl.when(tm > 0)
     def _():
         to_before.start()
 
-    @pl.when(tm < last)
-    def _():
-        to_next.start()
+    @pl.when(mc == 0)
+    def _():
+        greet()
+
+    loads[1].wait()
 
     @pl.when(tm == last)
     def _():
@@ -140,20 +161,15 @@
     @pl.when(tm == 0)
     def _():
         halo[1] = jnp.zeros((pairs, reach), jnp.float32)
-
-    loads[2].wait()
-    loads[3].wait()
-    transform([xv], fx)
-
-    loads[4].wait()
-    transform([yv], fy)
 
     lane = lax.broadcasted_iota(jnp.int32, (8, BLK), 1)
     sign = jnp.where(lane % 2 == 0, 1.0, -1.0).astype(jnp.float32)
 
     def take(ref, block, at):
-        rows = pl.ds(pl.multiple_of(block * pairs + at, 8), 8)
-        return ref[rows, 0:BLK], ref[rows, BLK : 2 * BLK]
+        return (
+            ref[block * half + at : block * half + at + 8, 0:BLK],
+            ref[block * half + at : block * half + at + 8, BLK : 2 * BLK],
+        )
 
     def turned(value):
         return -sign * value[1], sign * value[0]
@@ -161,78 +177,114 @@
     def plus(a, b):
         return b if a is None else (a[0] + b[0], a[1] + b[1])
 
-    def add(sums, q, a, b):
-        (ca, sa), (cb, sb) = a, b
-        sums[q] = plus(sums[q], (ca * cb + sa * sb, sa * cb - ca * sb))
-
-    def inner(at):
+    def left(x):
+        return x[0], x[0] - x[1], x[0] + x[1]
+
+    def right(z):
+        return z[0] + z[1], z[1], z[0]
+
+    def add(sums, q, x, z):
+        new = [u * v for u, v in zip(x, z)]
+        sums[q] = new if sums[q] is None else [u + v for u, v in zip(sums[q], new)]
+
+    def complex_of(sums):
+        return [(a - b, c - a) for a, b, c in sums]
+
+    def inner(xs_, ys_, at):
+        sums = [None] * extra
         window = {}
-        now = take(fy, 0, at)
+        now = take(ys_, 0, at)
         for j in range(blocks - 1):
-            ahead = take(fy, j + 1, at)
-            window[j] = plus(now, turned(ahead))
+            ahead = take(ys_, j + 1, at)
+            z = right(plus(now, turned(ahead)))
             now = ahead
-        sums = [None] * extra
-        for b in range(blocks - 1):
-            x = take(fx, b, at)
-            for q in range(extra):
-                if b + q < blocks - 1:
-                    add(sums, q, x, window[b + q])
-        return sums
-
-    def outer(at):
-        y = [take(fh, j, at) for j in range(near)]
-        window = [plus(take(fy, blocks - 1, at), turned(y[0]))]
+            window[j] = left(take(xs_, j, at))
+            for q in range(min(extra, j + 1)):
+                add(sums, q, window[j - q], z)
+        return complex_of(sums)
+
+    def outer(xs_, ys_, hs_, at):
+        y = [take(hs_, j, at) for j in range(near)]
+        window = [plus(take(ys_, blocks - 1, at), turned(y[0]))]
         window += [plus(y[j], turned(y[j + 1])) for j in range(near - 1)] + [y[near - 1]]
+        window = [right(z) for z in window]
         sums = [None] * extra
         for b in range(blocks - extra, blocks):
-            x = take(fx, b, at)
+            x = left(take(xs_, b, at))
             for q in range(extra):
                 if 0 <= b + q - (blocks - 1) <= near:
                     add(sums, q, x, window[b + q - (blocks - 1)])
         for b in range(near):
-            x = take(fh, near + b, at)
+            x = left(take(hs_, near + b, at))
             for q in range(extra):
                 j = b - near + q
                 if j >= near:
-                    add(sums, q, x, plus(take(fy, j, at), turned(take(fy, j + 1, at))))
+                    add(sums, q, x, right(plus(take(ys_, j, at), turned(take(ys_, j + 1, at)))))
                 elif j == near - 1:
-                    add(sums, q, x, turned(take(fy, near, at)))
-        return sums
-
-    @pl.loop(0, pairs // 8)
-    def _(g):
-        at = pl.multiple_of(g * 8, 8)
-        for q, (real, imag) in enumerate(inner(at)):
-            rows = pl.ds(pl.multiple_of(q * pairs + at, 8), 8)
-            res[rows, 0:BLK] = real
-            res[rows, BLK : 2 * BLK] = imag
+                    add(sums, q, x, right(turned(take(ys_, near, at))))
+        return complex_of(sums)
+
+    def inner_products(xs_, ys_, base):
+        for at in range(0, half, 8):
+            for q, (real, imag) in enumerate(inner(xs_, ys_, at)):
+                rows = slice(q * pairs + base + at, q * pairs + base + at + 8)
+                res[rows, 0:BLK] = real
+                res[rows, BLK : 2 * BLK] = imag
+
+    loads[2].wait()
+    loads[3].wait()
+    transform([xv.at[first]], px0, fx0)
+
+    @pl.when(jnp.logical_and(mc == 1, tm < last))
+    def _():
+        pl.semaphore_wait(told.at[1], 1)
 
     @pl.when(tm < last)
     def _():
+        to_next.start()
+
+    loads[4].wait()
+    loads[5].wait()
+    transform([yv.at[first]], py0, fy0)
+    transform([xv.at[second]], px1, fx1)
+    inner_products(fx0, fy0, 0)
+    transform([yv.at[second]], py1, fy1)
+    inner_products(fx1, fy1, half)
+
+    @pl.when(mc == 1)
+    def _():
+        pl.semaphore_wait(barrier, pairs * xs - own)
+        tell(2, tm - 1)
+
+    @pl.when(tm < last)
+    def _():
         to_before.wait_recv()
 
     @pl.when(tm > 0)
     def _():
         to_next.wait_recv()
 
-    transform([halo.at[0], halo.at[1]], fh)
-    for at in range(0, pairs, 8):
-        for q, (real, imag) in enumerate(outer(at)):
-            rows = slice(q * pairs + at, q * pairs + at + 8)
-            for half, value in enumerate((real, imag)):
-                columns = slice(half * BLK, (half + 1) * BLK)
-                high, low = high_low(res[rows, columns] + value)
-                rparts[rows, columns] = high.astype(jnp.float32)
-                rparts[extra * pairs + q * pairs + at : extra * pairs + q * pairs + at + 8, columns] = low.astype(jnp.float32)
-
-    loads[5].wait()
-    both = jnp.dot(rparts[...].astype(jnp.bfloat16), bwd[...], preferred_element_type=jnp.float32)
-    half = extra * pairs
-    lagged = (both[0:half, 0:BLK] + both[0:half, BLK : 2 * BLK]) + (
-        both[half:, 0:BLK] + both[half:, BLK : 2 * BLK]
+    transform([halo.at[0, first], halo.at[1, first]], ph0, fh0)
+    transform([halo.at[0, second], halo.at[1, second]], ph1, fh1)
+    for base, sources in ((0, (fx0, fy0, fh0)), (half, (fx1, fy1, fh1))):
+        for at in range(0, half, 8):
+            for q, values in enumerate(outer(*sources, at)):
+                rows = slice(q * pairs + base + at, q * pairs + base + at + 8)
+                under = slice(pairs * extra + rows.start, pairs * extra + rows.stop)
+                for part, value in enumerate(values):
+                    columns = slice(part * BLK, (part + 1) * BLK)
+                    rparts[rows, columns], rparts[under, columns] = high_low(res[rows, columns] + value)
+
+    both = jnp.dot(rparts[...], bwd[...], preferred_element_type=jnp.float32)
+    middle = extra * pairs
+    lagged = (both[0:middle, 0:BLK] + both[0:middle, BLK : 2 * BLK]) + (
+        both[middle:, 0:BLK] + both[middle:, BLK : 2 * BLK]
     )
-    send[...] = lagged.reshape(half, 1, BLK)
+    send[...] = lagged.reshape(middle, 1, BLK)
+
+    @pl.when(mc == 0)
+    def _():
+        pl.semaphore_wait(told.at[2], 1)
 
     def copy(row, q):
         return pltpu.make_async_remote_copy(
@@ -315,17 +367,18 @@
             pltpu.VMEM((2, pairs, L // 2), f32),
             pltpu.VMEM(fwd.shape, bf16),
             pltpu.VMEM(bwd.shape, bf16),
-            pltpu.VMEM((blocks * pairs, 2 * BLK), bf16),
-            pltpu.VMEM((blocks * pairs, N), f32),
-            pltpu.VMEM((blocks * pairs, N), f32),
+            *[pltpu.VMEM((blocks * pairs // 2, 2 * BLK), bf16)] * 4,
+            *[pltpu.VMEM((extra * pairs // 2, 2 * BLK), bf16)] * 2,
+            *[pltpu.VMEM((blocks * pairs // 2, N), f32)] * 4,
+            *[pltpu.VMEM((extra * pairs // 2, N), f32)] * 2,
             pltpu.VMEM((extra * pairs, N), f32),
-            pltpu.VMEM((extra * pairs, N), f32),
-            pltpu.VMEM((2 * extra * pairs, N), f32),
+            pltpu.VMEM((2 * extra * pairs, N), bf16),
             pltpu.VMEM((pairs * xs, 1, L // xs), f32),
             dma((7,)),
             dma((4,)),
             dma,
             dma,
+            pltpu.SemaphoreType.REGULAR((3,)),
         ],
         compiler_params=pltpu.CompilerParams(collective_id=0, has_side_effects=True),
     )(x_series, y_series, jnp.asarray(fwd), jnp.asarray(bwd))

time: 24 us -> 23.4 us (0.975)
  Pallas kernels: 23.3 us -> 22.6 us
    pallas_call x1, Pallas kernels: 23.3 us -> 22.6 us  [body(): pl.pallas_call(functools.partial(kernel, sizes), out_shape=pltpu.VMEM((2...]
where the time goes in v6:
time: 23.4 us; the launch traced here: 23.2 us
  Pallas kernels  22.6 us (97%)
  other arithmetic  0.66 us (3%)
    pallas_call x1, Pallas kernels, body(): pl.pallas_call(functools.partial(kernel, sizes), out_shape=pltpu.VMEM((2...  22.6 us
    reduce_sum x1, other arithmetic, body(): return jnp.sum(shares, axis=0)  0.66 us

profile of v6, /device:TPU:1, one launch (start us, length us, event | category | flops | bytes accessed | tf_op | source)
XLA Modules:
  0.0 23.2 jit_solution(17251293188443789941)
XLA Ops:
  0.0 22.6 %shard_map.46 = f32[128,1,128]{2,1,0:T(1,128)S(1)} custom-call(f32[32,4096]{1,0:T(8,128)} %x_hbm.1, f32[32,4096]{1,0:T(8,128)} %y_hbm.1, bf16[2,256,256]{2,1,0:T(8,128)(2,1)} %constant.6.clone.fwd_hbm, bf16[256,256]{1,0:T(8,128)(2,1)} %constant.7.clone.bwd_hbm), custom_call_target="tpu_custom_call" | custom-call | tf_op jit(solution)/shard_map/pallas_call | solution.py:358
  22.6 0.7 %reduce_sum.11 = f32[128]{0:T(128)} reduce(f32[128,1,128]{2,1,0:T(1,128)S(1)} %shard_map.46, f32[]{:T(128)} %constant.2.clone.1), dimensions={0,1}, to_apply=%region_0.0 | reduce | flops 16256 | bytes 66052 | tf_op jit(solution)/shard_map/reduce_sum | solution.py:385

commit v7 on v6

--- a/solution.py
+++ b/solution.py
@@ -43,15 +43,13 @@
 
 def kernel(
     sizes, x_hbm, y_hbm, fwd_hbm, bwd_hbm, recv,
-    xv, yv, edges, halo, fwd, bwd,
-    px0, px1, py0, py1, ph0, ph1, fx0, fx1, fy0, fy1, fh0, fh1, res, rparts, send,
+    xv, yv, lead, head, fwd, bwd,
+    px0, px1, py0, py1, ph0, ph1, fx0, fx1, fy0, fy1, fh0, fh1, res0, res1, split0, split1, send,
     load_sem, halo_sem, send_sem, recv_sem, told,
 ):
     zs, ys, xs = sizes
     pairs, length = xv.shape
     blocks, extra = length // BLK, L // BLK
-    near = extra // 2
-    reach = near * BLK
     half = pairs // 2
     first, second = slice(0, half), slice(half, pairs)
     group = 2 * ys
@@ -65,8 +63,7 @@
     own = jnp.where(source_x == mx, 1, 0)
 
     loads = [
-        pltpu.make_async_copy(y_hbm.at[:, 0:reach], edges.at[0], load_sem.at[0]),
-        pltpu.make_async_copy(x_hbm.at[:, length - reach : length], edges.at[1], load_sem.at[6]),
+        pltpu.make_async_copy(y_hbm.at[:, 0:L], lead, load_sem.at[0]),
         pltpu.make_async_copy(x_hbm, xv, load_sem.at[1]),
         pltpu.make_async_copy(fwd_hbm, fwd, load_sem.at[2]),
         pltpu.make_async_copy(y_hbm, yv, load_sem.at[3]),
@@ -116,27 +113,20 @@
             rows, fwd[1], preferred_element_type=jnp.float32
         )
 
-    def swap(side, other):
-        return pltpu.make_async_remote_copy(
-            src_ref=edges.at[side],
-            dst_ref=halo.at[side],
-            send_sem=halo_sem.at[side],
-            recv_sem=halo_sem.at[2 + side],
-            device_id=(other, mx),
-            device_id_type=MESH,
-        )
-
-    to_before, to_next = swap(0, jnp.maximum(tm - 1, 0)), swap(1, jnp.minimum(tm + 1, last))
+    to_before = pltpu.make_async_remote_copy(
+        src_ref=lead,
+        dst_ref=head,
+        send_sem=halo_sem.at[0],
+        recv_sem=halo_sem.at[1],
+        device_id=(jnp.maximum(tm - 1, 0), mx),
+        device_id_type=MESH,
+    )
 
     @pl.when(mc == 0)
     def _():
         pl.semaphore_wait(barrier, 1 + jnp.where(tm > 0, 1, 0))
         tell(0, tm + 1)
 
-    @pl.when(jnp.logical_and(mc == 0, tm > 0))
-    def _():
-        tell(1, tm - 1)
-
     @pl.when(mc == 1)
     def _():
         greet()
@@ -152,15 +142,9 @@
     def _():
         greet()
 
-    loads[1].wait()
-
     @pl.when(tm == last)
     def _():
-        halo[0] = jnp.zeros((pairs, reach), jnp.float32)
-
-    @pl.when(tm == 0)
-    def _():
-        halo[1] = jnp.zeros((pairs, reach), jnp.float32)
+        head[...] = jnp.zeros_like(head)
 
     lane = lax.broadcasted_iota(jnp.int32, (8, BLK), 1)
     sign = jnp.where(lane % 2 == 0, 1.0, -1.0).astype(jnp.float32)
@@ -204,87 +188,64 @@
         return complex_of(sums)
 
     def outer(xs_, ys_, hs_, at):
-        y = [take(hs_, j, at) for j in range(near)]
-        window = [plus(take(ys_, blocks - 1, at), turned(y[0]))]
-        window += [plus(y[j], turned(y[j + 1])) for j in range(near - 1)] + [y[near - 1]]
-        window = [right(z) for z in window]
+        y = [take(ys_, blocks - 1, at)] + [take(hs_, j, at) for j in range(extra)]
+        window = [right(plus(y[j], turned(y[j + 1]))) for j in range(extra)]
         sums = [None] * extra
         for b in range(blocks - extra, blocks):
             x = left(take(xs_, b, at))
             for q in range(extra):
-                if 0 <= b + q - (blocks - 1) <= near:
+                if b + q >= blocks - 1:
                     add(sums, q, x, window[b + q - (blocks - 1)])
-        for b in range(near):
-            x = left(take(hs_, near + b, at))
-            for q in range(extra):
-                j = b - near + q
-                if j >= near:
-                    add(sums, q, x, right(plus(take(ys_, j, at), turned(take(ys_, j + 1, at)))))
-                elif j == near - 1:
-                    add(sums, q, x, right(turned(take(ys_, near, at))))
         return complex_of(sums)
 
-    def inner_products(xs_, ys_, base):
+    def inner_products(xs_, ys_, into):
         for at in range(0, half, 8):
             for q, (real, imag) in enumerate(inner(xs_, ys_, at)):
-                rows = slice(q * pairs + base + at, q * pairs + base + at + 8)
-                res[rows, 0:BLK] = real
-                res[rows, BLK : 2 * BLK] = imag
-
+                rows = slice(q * half + at, q * half + at + 8)
+                into[rows, 0:BLK] = real
+                into[rows, BLK : 2 * BLK] = imag
+
+    loads[1].wait()
     loads[2].wait()
+    transform([xv.at[first]], px0, fx0)
+
     loads[3].wait()
-    transform([xv.at[first]], px0, fx0)
-
-    @pl.when(jnp.logical_and(mc == 1, tm < last))
-    def _():
-        pl.semaphore_wait(told.at[1], 1)
-
-    @pl.when(tm < last)
-    def _():
-        to_next.start()
-
     loads[4].wait()
-    loads[5].wait()
     transform([yv.at[first]], py0, fy0)
     transform([xv.at[second]], px1, fx1)
-    inner_products(fx0, fy0, 0)
+    inner_products(fx0, fy0, res0)
     transform([yv.at[second]], py1, fy1)
-    inner_products(fx1, fy1, half)
+    inner_products(fx1, fy1, res1)
 
     @pl.when(mc == 1)
     def _():
         pl.semaphore_wait(barrier, pairs * xs - own)
-        tell(2, tm - 1)
+        tell(1, tm - 1)
 
     @pl.when(tm < last)
     def _():
         to_before.wait_recv()
 
-    @pl.when(tm > 0)
-    def _():
-        to_next.wait_recv()
-
-    transform([halo.at[0, first], halo.at[1, first]], ph0, fh0)
-    transform([halo.at[0, second], halo.at[1, second]], ph1, fh1)
-    for base, sources in ((0, (fx0, fy0, fh0)), (half, (fx1, fy1, fh1))):
+    def finish(base, xs_, ys_, edge, part, hs_, sums, split):
+        transform(edge, part, hs_)
+        middle = extra * half
         for at in range(0, half, 8):
-            for q, values in enumerate(outer(*sources, at)):
-                rows = slice(q * pairs + base + at, q * pairs + base + at + 8)
-                under = slice(pairs * extra + rows.start, pairs * extra + rows.stop)
-                for part, value in enumerate(values):
-                    columns = slice(part * BLK, (part + 1) * BLK)
-                    rparts[rows, columns], rparts[under, columns] = high_low(res[rows, columns] + value)
-
-    both = jnp.dot(rparts[...], bwd[...], preferred_element_type=jnp.float32)
-    middle = extra * pairs
-    lagged = (both[0:middle, 0:BLK] + both[0:middle, BLK : 2 * BLK]) + (
-        both[middle:, 0:BLK] + both[middle:, BLK : 2 * BLK]
-    )
-    send[...] = lagged.reshape(middle, 1, BLK)
-
-    @pl.when(mc == 0)
-    def _():
-        pl.semaphore_wait(told.at[2], 1)
+            for q, values in enumerate(outer(xs_, ys_, hs_, at)):
+                rows = slice(q * half + at, q * half + at + 8)
+                under = slice(middle + rows.start, middle + rows.stop)
+                for which, value in enumerate(values):
+                    columns = slice(which * BLK, (which + 1) * BLK)
+                    split[rows, columns], split[under, columns] = high_low(
+                        sums[rows, columns] + value
+                    )
+        both = jnp.dot(split[...], bwd[...], preferred_element_type=jnp.float32)
+        lagged = (both[0:middle, 0:BLK] + both[0:middle, BLK : 2 * BLK]) + (
+            both[middle:, 0:BLK] + both[middle:, BLK : 2 * BLK]
+        )
+        for q in range(extra):
+            send[q * pairs + base : q * pairs + base + half] = lagged[
+                q * half : (q + 1) * half
+            ].reshape(half, 1, BLK)
 
     def copy(row, q):
         return pltpu.make_async_remote_copy(
@@ -297,15 +258,25 @@
         )
 
     own_at = jnp.where(own == 1, tm, -1)
-    for e in range(depth):
+    def send_rows(rows):
         for y in range(ys):
-            for c in (1, 0):
-                row = e * group + y * 2 + c
-                for q in range(xs):
-
-                    @pl.when(own_at != q * pairs + row)
-                    def _():
-                        copy(row, q).start()
+            for row in rows:
+                if row // 2 % ys == y:
+                    for q in range(xs):
+
+                        @pl.when(own_at != q * pairs + row)
+                        def _():
+                            copy(row, q).start()
+
+    finish(0, fx0, fy0, [head.at[first]], ph0, fh0, res0, split0)
+
+    @pl.when(mc == 0)
+    def _():
+        pl.semaphore_wait(told.at[1], 1)
+
+    send_rows(range(half - 1, -1, -1))
+    finish(half, fx1, fy1, [head.at[second]], ph1, fh1, res1, split1)
+    send_rows(range(pairs - 1, half - 1, -1))
 
     kept = pltpu.make_async_copy(send.at[tm], recv.at[tm], load_sem.at[5])
 
@@ -336,10 +307,6 @@
     @pl.when(tm > 0)
     def _():
         to_before.wait_send()
-
-    @pl.when(tm < last)
-    def _():
-        to_next.wait_send()
 
     for own_too in (0, 1):
 
@@ -363,22 +330,22 @@
         scratch_shapes=[
             pltpu.VMEM((pairs, length), f32),
             pltpu.VMEM((pairs, length), f32),
-            pltpu.VMEM((2, pairs, L // 2), f32),
-            pltpu.VMEM((2, pairs, L // 2), f32),
+            pltpu.VMEM((pairs, L), f32),
+            pltpu.VMEM((pairs, L), f32),
             pltpu.VMEM(fwd.shape, bf16),
             pltpu.VMEM(bwd.shape, bf16),
             *[pltpu.VMEM((blocks * pairs // 2, 2 * BLK), bf16)] * 4,
             *[pltpu.VMEM((extra * pairs // 2, 2 * BLK), bf16)] * 2,
             *[pltpu.VMEM((blocks * pairs // 2, N), f32)] * 4,
             *[pltpu.VMEM((extra * pairs // 2, N), f32)] * 2,
-            pltpu.VMEM((extra * pairs, N), f32),
-            pltpu.VMEM((2 * extra * pairs, N), bf16),
+            *[pltpu.VMEM((extra * pairs // 2, N), f32)] * 2,
+            *[pltpu.VMEM((extra * pairs, N), bf16)] * 2,
             pltpu.VMEM((pairs * xs, 1, L // xs), f32),
-            dma((7,)),
-            dma((4,)),
+            dma((6,)),
+            dma((2,)),
             dma,
             dma,
-            pltpu.SemaphoreType.REGULAR((3,)),
+            pltpu.SemaphoreType.REGULAR((2,)),
         ],
         compiler_params=pltpu.CompilerParams(collective_id=0, has_side_effects=True),
     )(x_series, y_series, jnp.asarray(fwd), jnp.asarray(bwd))

time: 23.4 us -> 22 us (0.940)
  Pallas kernels: 22.6 us -> 21.2 us
    pallas_call x1, Pallas kernels: 22.6 us -> 21.2 us  [body(): pl.pallas_call(functools.partial(kernel, sizes), out_shape=pltpu.VMEM((2...]
where the time goes in v7:
time: 22 us; the launch traced here: 21.9 us
  Pallas kernels  21.2 us (96%)
  other arithmetic  0.66 us (3%)
    pallas_call x1, Pallas kernels, body(): pl.pallas_call(functools.partial(kernel, sizes), out_shape=pltpu.VMEM((2...  21.2 us
    reduce_sum x1, other arithmetic, body(): return jnp.sum(shares, axis=0)  0.66 us

profile of v7, /device:TPU:1, one launch (start us, length us, event | category | flops | bytes accessed | tf_op | source)
XLA Modules:
  0.0 21.9 jit_solution(10472454948984984286)
XLA Ops:
  0.0 21.2 %shard_map.46 = f32[128,1,128]{2,1,0:T(1,128)S(1)} custom-call(f32[32,4096]{1,0:T(8,128)} %x_hbm.1, f32[32,4096]{1,0:T(8,128)} %y_hbm.1, bf16[2,256,256]{2,1,0:T(8,128)(2,1)} %constant.6.clone.fwd_hbm, bf16[256,256]{1,0:T(8,128)(2,1)} %constant.7.clone.bwd_hbm), custom_call_target="tpu_custom_call" | custom-call | tf_op jit(solution)/shard_map/pallas_call | solution.py:325
  21.3 0.7 %reduce_sum.11 = f32[128]{0:T(128)} reduce(f32[128,1,128]{2,1,0:T(1,128)S(1)} %shard_map.46, f32[]{:T(128)} %constant.2.clone.1), dimensions={0,1}, to_apply=%region_0.0 | reduce | flops 16256 | bytes 66052 | tf_op jit(solution)/shard_map/reduce_sum | solution.py:352

commit v8 on v7

--- a/solution.py
+++ b/solution.py
@@ -122,6 +122,8 @@
         device_id_type=MESH,
     )
 
+    greet()
+
     @pl.when(mc == 0)
     def _():
         pl.semaphore_wait(barrier, 1 + jnp.where(tm > 0, 1, 0))
@@ -129,7 +131,6 @@
 
     @pl.when(mc == 1)
     def _():
-        greet()
         pl.semaphore_wait(told.at[0], 1)
 
     loads[0].wait()
@@ -137,10 +138,6 @@
     @pl.when(tm > 0)
     def _():
         to_before.start()
-
-    @pl.when(mc == 0)
-    def _():
-        greet()
 
     @pl.when(tm == last)
     def _():

time: 22 us -> 21.7 us (0.986)
  Pallas kernels: 21.2 us -> 20.9 us
    pallas_call x1, Pallas kernels: 21.2 us -> 20.9 us  [body(): pl.pallas_call(functools.partial(kernel, sizes), out_shape=pltpu.VMEM((2...]
where the time goes in v8:
time: 21.7 us; the launch traced here: 21.6 us
  Pallas kernels  20.9 us (96%)
  other arithmetic  0.66 us (3%)
    pallas_call x1, Pallas kernels, body(): pl.pallas_call(functools.partial(kernel, sizes), out_shape=pltpu.VMEM((2...  20.9 us
    reduce_sum x1, other arithmetic, body(): return jnp.sum(shares, axis=0)  0.66 us

profile of v8, /device:TPU:1, one launch (start us, length us, event | category | flops | bytes accessed | tf_op | source)
XLA Modules:
  0.0 21.6 jit_solution(13595022545969807183)
XLA Ops:
  0.0 20.9 %shard_map.46 = f32[128,1,128]{2,1,0:T(1,128)S(1)} custom-call(f32[32,4096]{1,0:T(8,128)} %x_hbm.1, f32[32,4096]{1,0:T(8,128)} %y_hbm.1, bf16[2,256,256]{2,1,0:T(8,128)(2,1)} %constant.6.clone.fwd_hbm, bf16[256,256]{1,0:T(8,128)(2,1)} %constant.7.clone.bwd_hbm), custom_call_target="tpu_custom_call" | custom-call | tf_op jit(solution)/shard_map/pallas_call | solution.py:322
  20.9 0.7 %reduce_sum.11 = f32[128]{0:T(128)} reduce(f32[128,1,128]{2,1,0:T(1,128)S(1)} %shard_map.46, f32[]{:T(128)} %constant.2.clone.1), dimensions={0,1}, to_apply=%region_0.0 | reduce | flops 16256 | bytes 66052 | tf_op jit(solution)/shard_map/reduce_sum | solution.py:349

commit v9 on v8

--- a/solution.py
+++ b/solution.py
@@ -113,14 +113,17 @@
             rows, fwd[1], preferred_element_type=jnp.float32
         )
 
-    to_before = pltpu.make_async_remote_copy(
-        src_ref=lead,
-        dst_ref=head,
-        send_sem=halo_sem.at[0],
-        recv_sem=halo_sem.at[1],
-        device_id=(jnp.maximum(tm - 1, 0), mx),
-        device_id_type=MESH,
-    )
+    to_before = [
+        pltpu.make_async_remote_copy(
+            src_ref=lead.at[rows],
+            dst_ref=head.at[rows],
+            send_sem=halo_sem.at[i],
+            recv_sem=halo_sem.at[2 + i],
+            device_id=(jnp.maximum(tm - 1, 0), mx),
+            device_id_type=MESH,
+        )
+        for i, rows in enumerate((first, second))
+    ]
 
     greet()
 
@@ -137,7 +140,8 @@
 
     @pl.when(tm > 0)
     def _():
-        to_before.start()
+        for part in to_before:
+            part.start()
 
     @pl.when(tm == last)
     def _():
@@ -218,10 +222,6 @@
     def _():
         pl.semaphore_wait(barrier, pairs * xs - own)
         tell(1, tm - 1)
-
-    @pl.when(tm < last)
-    def _():
-        to_before.wait_recv()
 
     def finish(base, xs_, ys_, edge, part, hs_, sums, split):
         transform(edge, part, hs_)
@@ -265,6 +265,10 @@
                         def _():
                             copy(row, q).start()
 
+    @pl.when(tm < last)
+    def _():
+        to_before[0].wait_recv()
+
     finish(0, fx0, fy0, [head.at[first]], ph0, fh0, res0, split0)
 
     @pl.when(mc == 0)
@@ -272,6 +276,10 @@
         pl.semaphore_wait(told.at[1], 1)
 
     send_rows(range(half - 1, -1, -1))
+    @pl.when(tm < last)
+    def _():
+        to_before[1].wait_recv()
+
     finish(half, fx1, fy1, [head.at[second]], ph1, fh1, res1, split1)
     send_rows(range(pairs - 1, half - 1, -1))
 
@@ -303,7 +311,8 @@
 
     @pl.when(tm > 0)
     def _():
-        to_before.wait_send()
+        for part in to_before:
+            part.wait_send()
 
     for own_too in (0, 1):
 
@@ -339,7 +348,7 @@
             *[pltpu.VMEM((extra * pairs, N), bf16)] * 2,
             pltpu.VMEM((pairs * xs, 1, L // xs), f32),
             dma((6,)),
-            dma((2,)),
+            dma((4,)),
             dma,
             dma,
             pltpu.SemaphoreType.REGULAR((2,)),

time: 21.7 us -> 21.3 us (0.982)
  Pallas kernels: 20.9 us -> 20.5 us
    pallas_call x1, Pallas kernels: 20.9 us -> 20.5 us  [body(): pl.pallas_call(functools.partial(kernel, sizes), out_shape=pltpu.VMEM((2...]
where the time goes in v9:
time: 21.3 us; the launch traced here: 21.2 us
  Pallas kernels  20.5 us (96%)
  other arithmetic  0.66 us (3%)
    pallas_call x1, Pallas kernels, body(): pl.pallas_call(functools.partial(kernel, sizes), out_shape=pltpu.VMEM((2...  20.5 us
    reduce_sum x1, other arithmetic, body(): return jnp.sum(shares, axis=0)  0.66 us

profile of v9, /device:TPU:1, one launch (start us, length us, event | category | flops | bytes accessed | tf_op | source)
XLA Modules:
  0.0 21.2 jit_solution(271889262297018898)
XLA Ops:
  0.0 20.5 %shard_map.46 = f32[128,1,128]{2,1,0:T(1,128)S(1)} custom-call(f32[32,4096]{1,0:T(8,128)} %x_hbm.1, f32[32,4096]{1,0:T(8,128)} %y_hbm.1, bf16[2,256,256]{2,1,0:T(8,128)(2,1)} %constant.6.clone.fwd_hbm, bf16[256,256]{1,0:T(8,128)(2,1)} %constant.7.clone.bwd_hbm), custom_call_target="tpu_custom_call" | custom-call | tf_op jit(solution)/shard_map/pallas_call | solution.py:331
  20.5 0.7 %reduce_sum.11 = f32[128]{0:T(128)} reduce(f32[128,1,128]{2,1,0:T(1,128)S(1)} %shard_map.46, f32[]{:T(128)} %constant.2.clone.1), dimensions={0,1}, to_apply=%region_0.0 | reduce | flops 16256 | bytes 66052 | tf_op jit(solution)/shard_map/reduce_sum | solution.py:358

commit v10 on v9

--- a/solution.py
+++ b/solution.py
@@ -63,14 +63,15 @@
     own = jnp.where(source_x == mx, 1, 0)
 
     loads = [
-        pltpu.make_async_copy(y_hbm.at[:, 0:L], lead, load_sem.at[0]),
+        pltpu.make_async_copy(y_hbm.at[first, 0:L], lead.at[first], load_sem.at[0]),
         pltpu.make_async_copy(x_hbm, xv, load_sem.at[1]),
         pltpu.make_async_copy(fwd_hbm, fwd, load_sem.at[2]),
         pltpu.make_async_copy(y_hbm, yv, load_sem.at[3]),
         pltpu.make_async_copy(bwd_hbm, bwd, load_sem.at[4]),
+        pltpu.make_async_copy(y_hbm.at[second, 0:L], lead.at[second], load_sem.at[6]),
     ]
-    for load in loads:
-        load.start()
+    for i in (0, 5, 1, 2, 3, 4):
+        loads[i].start()
 
     barrier = pltpu.get_barrier_semaphore()
 
@@ -136,11 +137,11 @@
     def _():
         pl.semaphore_wait(told.at[0], 1)
 
-    loads[0].wait()
-
-    @pl.when(tm > 0)
-    def _():
-        for part in to_before:
+    for load, part in ((loads[0], to_before[0]), (loads[5], to_before[1])):
+        load.wait()
+
+        @pl.when(tm > 0)
+        def _():
             part.start()
 
     @pl.when(tm == last)
@@ -347,7 +348,7 @@
             *[pltpu.VMEM((extra * pairs // 2, N), f32)] * 2,
             *[pltpu.VMEM((extra * pairs, N), bf16)] * 2,
             pltpu.VMEM((pairs * xs, 1, L // xs), f32),
-            dma((6,)),
+            dma((7,)),
             dma((4,)),
             dma,
             dma,

time: 21.3 us -> 21.3 us (level)
  no operation moved by 1% of the time
where the time goes in v10:
time: 21.3 us; the launch traced here: 21.2 us
  Pallas kernels  20.5 us (96%)
  other arithmetic  0.66 us (3%)
    pallas_call x1, Pallas kernels, body(): pl.pallas_call(functools.partial(kernel, sizes), out_shape=pltpu.VMEM((2...  20.5 us
    reduce_sum x1, other arithmetic, body(): return jnp.sum(shares, axis=0)  0.66 us

profile of v10, /device:TPU:1, one launch (start us, length us, event | category | flops | bytes accessed | tf_op | source)
XLA Modules:
  0.0 21.2 jit_solution(579997499580427565)
XLA Ops:
  0.0 20.5 %shard_map.46 = f32[128,1,128]{2,1,0:T(1,128)S(1)} custom-call(f32[32,4096]{1,0:T(8,128)} %x_hbm.1, f32[32,4096]{1,0:T(8,128)} %y_hbm.1, bf16[2,256,256]{2,1,0:T(8,128)(2,1)} %constant.6.clone.fwd_hbm, bf16[256,256]{1,0:T(8,128)(2,1)} %constant.7.clone.bwd_hbm), custom_call_target="tpu_custom_call" | custom-call | tf_op jit(solution)/shard_map/pallas_call | solution.py:332
  20.5 0.7 %reduce_sum.11 = f32[128]{0:T(128)} reduce(f32[128,1,128]{2,1,0:T(1,128)S(1)} %shard_map.46, f32[]{:T(128)} %constant.2.clone.1), dimensions={0,1}, to_apply=%region_0.0 | reduce | flops 16256 | bytes 66052 | tf_op jit(solution)/shard_map/reduce_sum | solution.py:359
